TPU v7x, 1024 devices: a whole 4x8x16 slice. The times are simulated.
1024 devices in a mesh: gx: 8 (over y), gy: 4 (over x_lo, core), gz: 32 (over z, x_hi).
Axes of the slice: x: 4 (x_hi: 2, x_lo: 2; x = x_hi * 2 + x_lo), y: 8, z: 16, core: 2. Of those that a mesh axis runs over, the one named last changes fastest.
Arguments:
- rhs_velocity: float32 [3, 32, 32, 4096], P(None, 'gx', 'gy', 'gz'), may hold values from -6 to 6
- rhs_pressure: float32 [32, 32, 4096], P('gx', 'gy', 'gz'), may hold values from -6 to 6
- layer_ids: int32 [32, 32, 4096], P('gx', 'gy', 'gz'), may hold values from 0 to 7
- visc_table: float32 [8], replicated, may hold values from 0.5 to 8
- stencil: float32 [27, 3, 3], replicated, as said below
Outputs:
- velocity_out: float32 [3, 32, 32, 4096], P(None, 'gx', 'gy', 'gz')
- pressure_out: float32 [32, 32, 4096], P('gx', 'gy', 'gz')
Inputs may be any that keep to these rules, and one draw needn't show every extreme that they name: The block stencil[13] has a positive diagonal that dominates its row together with all other blocks' entries.
All inputs are finite; a program needn't handle non-finite values.
Results may differ from a plain program's by a relative error of at most 0.00015.
Values sent between devices are 32-bit elements; how exact they have to be, the bound alone decides.
A program may use at most 32 MiB of HBM per device.

v0:
```python
import functools

import numpy as np
import jax
import jax.numpy as jnp
from jax import lax
from jax.experimental import pallas as pl
from jax.experimental.pallas import tpu as pltpu
from jax.sharding import PartitionSpec as P

F32 = jnp.float32
BF16 = jnp.bfloat16
MESH = pl.DeviceIdType.MESH

THETA = (1.8 + 0.2) / 2.0
DELTA = (1.8 - 0.2) / 2.0
SIGMA = THETA / DELTA
RHO0 = 1.0 / SIGMA
RHO1 = 1.0 / (2.0 * SIGMA - RHO0)
MOM = RHO1 * RHO0
WEIGHT = 2.0 * RHO1 / DELTA

XLO, XHI, YLO, YHI, ZLO, ZHI, NEVER = 1, 2, 4, 8, 16, 32, 64

ONE, ZERO = 28, 31

CORNER_X = (4, 5, -2, -1)
SIDES = [(dx, dy) for dx in (-1, 0, 1) for dy in (-1, 0, 1) if (dx, dy) != (0, 0)]


def plane_block(x, j):
    return [(x, r, j) for r in range(8)]


def y_block(s, j):
    return [(r // 2, (-2 if s == 0 else 8) + r % 2, j) for r in range(8)]


def c_block(s, j):
    return [(CORNER_X[r // 2], (-2 if s == 0 else 8) + r % 2, j) for r in range(8)]


def yh_block(i, xs=range(4)):
    return [(r // 2, -1 if r % 2 else 8, i) if r // 2 in xs else None for r in range(8)]


def ch_block(i, xs=(-1, 4)):
    return [(CORNER_X[r // 2], -1 if r % 2 else 8, i) if CORNER_X[r // 2] in xs else None for r in range(8)]


def rows_wide(comps):
    rows = []
    for x in (-2, -1, 0, 1, 2):
        for j in range(comps):
            rows += plane_block(x, j)
    for block in (y_block, c_block):
        for s in range(2):
            for j in range(comps):
                rows += block(s, j)
    for x in (3, 4, 5):
        for j in range(comps):
            rows += plane_block(x, j)
    return rows


def rows_ring(comps):
    rows = []
    for x in range(-1, 5):
        for i in range(comps):
            rows += plane_block(x, i)
    for i in range(comps):
        rows += yh_block(i)
    for i in range(comps):
        rows += ch_block(i)
    return rows


def rows_half(planes, y_xs, c_xs):
    rows = []
    for x in planes:
        for i in range(3):
            rows += plane_block(x, i)
    for i in range(3):
        rows += yh_block(i, y_xs)
    for i in range(3):
        rows += ch_block(i, c_xs)
    return rows + [None] * 8


def rows_coarse_in():
    rows = []
    for dx in (-1, 0, 1):
        for dy in (-1, 0, 1):
            for j in range(3):
                rows += [(2 * dx + r // 4, 4 * dy + r % 4, j) for r in range(8)]
    return rows


def rows_coarse_out():
    rows = []
    for q in range(3):
        for i in range(3):
            for r in range(8):
                n = 8 * q + r
                rows.append((n // 6 - 1, n % 6 - 1, i))
    return rows + [None] * 8


def index_stencil(outs, ins):
    table = np.full((len(outs), 256), ZERO, np.int32)
    for m, out in enumerate(outs):
        if out is None:
            continue
        for k, source in enumerate(ins):
            if source is None:
                continue
            a, b = source[0] - out[0] + 1, source[1] - out[1] + 1
            if 0 <= a <= 2 and 0 <= b <= 2:
                table[m, k] = 3 * (3 * a + b) + source[2]
    return table


def index_same(outs, ins, scale):
    table = np.full((len(outs), 256), ZERO, np.int32)
    for m, out in enumerate(outs):
        if out is None:
            continue
        for k, source in enumerate(ins):
            if source is not None and (out[0] // scale, out[1] // scale, out[2]) == source:
                table[m, k] = ONE
    return table


def index_refined(outs, ins):
    table = np.full((len(outs), 256), ZERO, np.int32)
    for m, out in enumerate(outs):
        if out is None:
            continue
        for k, source in enumerate(ins):
            if source is None:
                continue
            a = [v for v in range(3) if (out[0] + v - 1) // 2 == source[0]]
            b = [v for v in range(3) if (out[1] + v - 1) // 2 == source[1]]
            if a and b:
                segment = (len(a) - 1) + 2 * (len(b) - 1)
                table[m, k] = 32 * segment + 3 * (3 * a[0] + b[0]) + source[2]
    return table


def codes(rows, x_end, y_end, lanes, z_bits):
    table = np.full((len(rows), lanes), NEVER, np.int32)
    z_row = np.full((lanes,), NEVER, np.int32)
    for lane, bits in z_bits:
        z_row[lane] = bits
    for m, row in enumerate(rows):
        if row is None:
            continue
        bits = (XLO if row[0] < 0 else 0) | (XHI if row[0] >= x_end else 0)
        bits |= (YLO if row[1] < 0 else 0) | (YHI if row[1] >= y_end else 0)
        table[m] = bits | z_row
    return table


def face_matrix(outs, ins):
    table = np.zeros((len(outs), len(ins)), np.float32)
    for m, out in enumerate(outs):
        if out is None:
            continue
        for k, source in enumerate(ins):
            if source is not None and abs(source[0] - out[0]) + abs(source[1] - out[1]) == 1:
                table[m, k] = 1.0
    return table


FINE_LANES = [(z, 0) for z in range(128)]
WIDE_Z = FINE_LANES + [(128, ZHI), (129, ZHI), (254, ZLO), (255, ZLO)]
RING_Z = FINE_LANES + [(128, ZHI), (255, ZLO)]
COARSE_Z = [(z, 0) for z in range(64)] + [(64, ZHI), (65, ZHI), (126, ZLO), (127, ZLO)]
COARSE_RING_Z = [(z, 0) for z in range(64)] + [(64, ZHI), (127, ZLO)]

WIDE = rows_wide(3)
RING = rows_ring(3)
LOCAL = [row for x in range(4) for i in range(3) for row in plane_block(x, i)]
HALF_A = rows_half((-1, 0, 1), (0, 1), (-1,))
HALF_B = rows_half((2, 3, 4), (2, 3), (4,))
COARSE_IN = rows_coarse_in()
COARSE_OUT = rows_coarse_out()

SECTIONS = [
    ("a", index_stencil(HALF_A, WIDE[0:256]), 3),
    ("b", index_stencil(HALF_B, WIDE[32:288]), 3),
    ("local", index_stencil(LOCAL, RING), 3),
    ("coarse", index_stencil(COARSE_OUT, COARSE_IN), 3),
    ("keep", index_same(COARSE_OUT, COARSE_IN, 1), 1),
    ("fine", index_refined(RING, COARSE_OUT), 3),
    ("spread", index_same(RING, COARSE_OUT, 2), 1),
]
INDEX = np.concatenate([section[1] for section in SECTIONS], axis=0)
PLACE = {}
_at = 0
_row = 0
for _name, _table, _copies in SECTIONS:
    PLACE[_name] = (_at, _row, len(_table), _copies)
    _at += len(_table)
    _row += len(_table) * _copies
W_ROWS = _row

CODE_WIDE = codes(WIDE, 4, 8, 256, WIDE_Z)
CODE_RING = codes(RING, 4, 8, 256, RING_Z)
CODE_COARSE = codes(COARSE_IN, 2, 4, 128, COARSE_Z)
CODE_COARSE_RING = codes(COARSE_OUT, 2, 4, 128, COARSE_RING_Z)
CODE_WIDE_P = codes(rows_wide(1), 4, 8, 256, WIDE_Z)
CODE_RING_P = codes(rows_ring(1), 4, 8, 256, RING_Z)
CODE_256 = np.concatenate([CODE_WIDE, CODE_RING, CODE_WIDE_P, CODE_RING_P], axis=0)
CODE_128 = np.concatenate([CODE_COARSE, CODE_COARSE_RING], axis=0)


def face_pair(outs, ins, width, total):
    single = face_matrix(outs, ins)
    table = np.zeros((len(outs), total), np.float32)
    table[:, : single.shape[1]] = single
    table[:, width : width + single.shape[1]] = single
    return table


FACE_1 = face_pair(rows_ring(1), rows_wide(1), 128, 256)
FACE_2 = face_pair([row for x in range(4) for row in plane_block(x, 0)], rows_ring(1), 64, 128)


def split(value):
    high = value.astype(BF16)
    low = (value - high.astype(F32)).astype(BF16)
    return high, low


def z_shift_sum(product, rows):
    lanes = product.shape[1]
    return (
        product[rows : 2 * rows]
        + pltpu.roll(product[0:rows], 1, 1)
        + pltpu.roll(product[2 * rows : 3 * rows], lanes - 1, 1)
    )


def body(
    rhs_hbm, press_hbm, ids_hbm, visc_hbm, stencil_hbm, index_hbm, code256_hbm, code128_hbm, face1_hbm, face2_hbm,
    out_ref, pout_ref,
    rhs, press, ids, visc, stencil, index, code256, code128, face1, face2,
    eta, main, ypack, zpack, zmerged, rx, ry, rz, rf,
    main2, ypack2, zpack2, zmerged2, rx2, ry2, rz2, rf2,
    cmain, czpack, czmerged, rc, rcz, rcf,
    tables, w, w_fine, wide, wide_p, ring_u, ring_x2, ring_t, resid, ceta,
    in_sem, send_sem, recv_sem,
):
    nx, ny, nz = (lax.axis_size(name) for name in ("gx", "gy", "gz"))
    ix, iy, iz = (lax.axis_index(name) for name in ("gx", "gy", "gz"))

    def device(dx, dy, dz):
        return (
            lax.rem(ix + dx + nx, nx),
            lax.rem(iy + dy + ny, ny),
            lax.rem(iz + dz + nz, nz),
        )

    barrier = pltpu.get_barrier_semaphore()
    for dz in (-1, 1):
        pl.semaphore_signal(barrier, inc=1, device_id=device(0, 0, dz), device_id_type=MESH)
    for dx, dy in SIDES:
        pl.semaphore_signal(barrier, inc=1, device_id=device(dx, dy, 0), device_id_type=MESH)

    loads = [
        pltpu.make_async_copy(source, target, in_sem.at[n])
        for n, (source, target) in enumerate(
            [
                (visc_hbm, visc),
                (ids_hbm, ids),
                (rhs_hbm, rhs),
                (press_hbm, press),
                (stencil_hbm, stencil),
                (index_hbm, index),
                (code256_hbm, code256),
                (code128_hbm, code128),
                (face1_hbm, face1),
                (face2_hbm, face2),
            ]
        )
    ]
    for load in loads:
        load.start()

    counter = [0]
    sent = []

    def send(source, target, where):
        n = counter[0]
        counter[0] += 1
        copy = pltpu.make_async_remote_copy(
            src_ref=source,
            dst_ref=target,
            send_sem=send_sem.at[n],
            recv_sem=recv_sem.at[n],
            device_id=device(*where),
            device_id_type=MESH,
        )
        copy.start()
        sent.append(copy)
        return copy

    bad = (
        NEVER
        + XLO * (ix == 0).astype(jnp.int32)
        + XHI * (ix == nx - 1).astype(jnp.int32)
        + YLO * (iy == 0).astype(jnp.int32)
        + YHI * (iy == ny - 1).astype(jnp.int32)
        + ZLO * (iz == 0).astype(jnp.int32)
        + ZHI * (iz == nz - 1).astype(jnp.int32)
    )

    lane8 = lax.broadcasted_iota(jnp.int32, (8, 128), 1)
    row8 = lax.broadcasted_iota(jnp.int32, (8, 128), 0)

    def inside(code):
        return (code & bad) == 0

    for load in loads[:4]:
        load.wait()
    for p in range(4):
        layer = ids[p]
        value = jnp.zeros((8, 128), F32)
        for k in range(8):
            value = value + jnp.where(layer == k, visc[k], 0.0)
        eta[p] = value
        inverse = 1.0 / value
        for j in range(3):
            main[p, j] = rhs[j, p] * inverse
        main[p, 3] = press[p] * value

    def pack_y(source, target, comps):
        for s in range(2):
            for j in range(comps):
                for p in range(4):
                    target[s, j, 2 * p : 2 * p + 2, :] = source[p, j, 6 * s : 6 * s + 2, :]

    def item_window(k):
        return ((lane8 + (130 - 4 * k)) & 127) < 4

    def pack_z(source, packed, comps):
        total = jnp.zeros((8, 128), F32)
        k = 0
        for p in range(4):
            for j in range(comps):
                total = jnp.where(item_window(k), pltpu.roll(source[p, j], 4 * k, 1), total)
                k += 1
        for s in range(2):
            for j in range(comps):
                total = jnp.where(item_window(k), pltpu.roll(packed[s, j], 4 * k, 1), total)
                k += 1
        return total

    def tile_edge(merged, k):
        moved = pltpu.roll(merged, (128 - 4 * k) % 128, 1)
        return moved

    pack_y(main, ypack, 4)
    zpack[...] = pack_z(main, ypack, 4)

    pl.semaphore_wait(barrier, 10)

    def send_faces(source, packed, x_slots, y_slots):
        copies = []
        for dx in (-1, 1):
            planes = source.at[pl.ds(0 if dx < 0 else 2, 2)]
            copies.append(send(planes, x_slots.at[0 if dx > 0 else 1], (dx, 0, 0)))
        for dy in (-1, 1):
            for dx in (0, -1, 1):
                copies.append(
                    send(packed.at[0 if dy < 0 else 1], y_slots.at[0 if dy > 0 else 1, dx + 1], (dx, dy, 0))
                )
        return copies

    def send_sides(source, slots):
        return [send(source, slots.at[n], (dx, dy, 0)) for n, (dx, dy) in enumerate(SIDES)]

    def send_z(source, slots):
        return [send(source, slots.at[0 if dz > 0 else 1], (0, 0, dz)) for dz in (-1, 1)]

    z_first = send_z(zpack, rz)
    faces_first = send_faces(main, ypack, rx, ry)

    lane16 = lax.broadcasted_iota(jnp.int32, (16, 128), 1)
    loads[4].wait()
    kc = (stencil[0, 0, 13] + stencil[1, 1, 13] + stencil[2, 2, 13]) / 3.0
    loads[5].wait()
    for c in range(3):
        rows = []
        for i in range(3):
            base = jnp.zeros((8, 128), F32)
            for a in range(3):
                for b in range(3):
                    for j in range(3):
                        at = 3 * (3 * a + b) + j
                        base = jnp.where(lane8 == at, stencil[i, j, 9 * a + 3 * b + c], base)
            low = lane8 < 27
            pair_a = base + jnp.where(low, pltpu.roll(base, 128 - 9, 1), 0.0)
            pair_b = base + jnp.where(low, pltpu.roll(base, 128 - 3, 1), 0.0)
            pair_ab = pair_a + jnp.where(low, pltpu.roll(pair_a, 128 - 3, 1), 0.0)
            full = base + pltpu.roll(pair_a, 32, 1) + pltpu.roll(pair_b, 64, 1) + pltpu.roll(pair_ab, 96, 1)
            rows.append(jnp.where(lane8 == ONE, 1.0, full))
        for combo, (one, two) in enumerate(((0, 1), (2, 0), (1, 2))):
            tables[3 * c + combo, 0:8, :] = rows[one]
            tables[3 * c + combo, 8:16, :] = rows[two]

    def build(name, target, base, tiles, width):
        at, _, count, copies = PLACE[name]

        def step(t, carry):
            combo = lax.rem(t, 3)
            start = pl.multiple_of(t * 16, 16)
            for tile in range(tiles):
                picked = index[pl.ds(at + start, 16), 128 * tile : 128 * tile + 128]
                for c in range(copies):
                    value = jnp.take_along_axis(
                        tables[3 * c + combo], picked, axis=1, mode="promise_in_bounds"
                    )
                    high, low = split(value)
                    rows = pl.ds(base + c * count + start, 16)
                    target[rows, 128 * tile : 128 * tile + 128] = high
                    target[rows, width + 128 * tile : width + 128 * tile + 128] = low
                    target[rows, 2 * width + 128 * tile : 2 * width + 128 * tile + 128] = high
            return carry

        lax.fori_loop(0, count // 16, step, 0)

    def w_base(name):
        return PLACE[name][1]

    fine_base = w_base("fine")
    for name in ("a", "b", "local"):
        build(name, w, w_base(name), 2, 256)

    def merge_z(slots):
        return jnp.where((lane8 & 3) < 2, slots[1], slots[0])

    for copy in z_first:
        copy.wait_recv()
    zmerged[...] = merge_z(rz)
    sides_first = send_sides(zmerged, rf)

    for name in ("coarse", "keep"):
        build(name, w, w_base(name), 2, 256)
    for name in ("fine", "spread"):
        build(name, w_fine, w_base(name) - fine_base, 1, 128)

    for load in loads[6:]:
        load.wait()

    for copy in faces_first:
        copy.wait_recv()
    for copy in sides_first:
        copy.wait_recv()

    side = {offset: n for n, offset in enumerate(SIDES)}

    def wide_blocks(comp, comps, source, x_slots, y_slots, merged, forwarded):
        first_y = 4 * comps

        def edge(block, k):
            return tile_edge(block, k)

        def from_side(dx, dy):
            return forwarded[side[(-dx, -dy)]]

        blocks = {}
        for p in range(4):
            blocks[p] = (source[p, comp], edge(merged[...], p * comps + comp))
        for n in range(2):
            blocks[n - 2] = (x_slots[0, n, comp], edge(from_side(-1, 0), (n + 2) * comps + comp))
            blocks[n + 4] = (x_slots[1, n, comp], edge(from_side(1, 0), n * comps + comp))
        low_rows = (row8 & 7) < 4
        for s, dy in enumerate((-1, 1)):
            k = first_y + (1 - s) * comps + comp
            blocks["y", s] = (y_slots[s, 1, comp], edge(from_side(0, dy), k))
            above = (y_slots[s, 0, comp], edge(from_side(1, dy), k))
            below = (y_slots[s, 2, comp], edge(from_side(-1, dy), k))
            blocks["c", s] = tuple(jnp.where(low_rows, one, two) for one, two in zip(above, below))
        return blocks

    def store_wide(target, comps, comp_list, code_at, source, x_slots, y_slots, merged, forwarded):
        count = len(comp_list)
        for place, comp in enumerate(comp_list):
            blocks = wide_blocks(comp, comps, source, x_slots, y_slots, merged, forwarded)
            order = [-2, -1, 0, 1, 2]
            at = {}
            for n, x in enumerate(order):
                at[x] = n * count + place
            for n in range(2):
                at["y", n] = (5 + n) * count + place
                at["c", n] = (7 + n) * count + place
            for n, x in enumerate((3, 4, 5)):
                at[x] = (9 + n) * count + place
            for key, n in at.items():
                one, two = blocks[key]
                rows = slice(8 * n, 8 * n + 8)
                code = slice(code_at + 8 * n, code_at + 8 * n + 8)
                target[rows, 0:128] = jnp.where(inside(code256[code, 0:128]), one, 0.0)
                target[rows, 128:256] = jnp.where(inside(code256[code, 128:256]), two, 0.0)

    def ring_of(source, comps):
        def block(n):
            return source[8 * comps * n : 8 * comps * (n + 1), :]

        rows = 8 * comps
        local_row = lax.broadcasted_iota(jnp.int32, (rows, 256), 0)
        odd = (local_row & 1) == 1
        return jnp.concatenate(
            [
                block(1), block(2), block(3), block(4), block(9), block(10),
                jnp.where(odd, block(5), block(6)),
                jnp.where(odd, block(7), block(8)),
            ],
            axis=0,
        )

    def operator_ring():
        parts = []
        for name, start in (("a", 0), ("b", 32)):
            high, low = split(wide[start : start + 256, :])
            right = jnp.concatenate([high, high, low], axis=0)
            base = w_base(name)
            product = jnp.dot(w[base : base + 384, :], right, preferred_element_type=F32)
            parts.append(z_shift_sum(product, 128))
        one, two = parts
        return jnp.concatenate([one[0:72], two[0:72], one[72:120] + two[72:120]], axis=0)

    def operator_local(value):
        high, low = split(value)
        gap = jnp.zeros((64, 256), BF16)
        right = jnp.concatenate([high, gap, high, gap, low, gap], axis=0)
        base = w_base("local")
        product = jnp.dot(w[base : base + 288, :], right, preferred_element_type=F32)
        return z_shift_sum(product, 96)

    ikc = jnp.full((8, 256), 1.0, F32) / kc
    ikc = ikc[0:1, :]
    gain_u = ((1.0 + MOM + WEIGHT * THETA) / THETA) * ikc
    gain_s = (-WEIGHT / THETA) * ikc * ikc

    ring_code = len(CODE_WIDE)
    wide_p_code = ring_code + len(CODE_RING)
    ring_p_code = wide_p_code + len(CODE_WIDE_P)

    def ring_inside():
        return inside(code256[ring_code : ring_code + 192, :])

    store_wide(wide, 4, (0, 1, 2), 0, main, rx, ry, zmerged, rf)
    u_ring = ring_of(wide, 3)
    ring_u[...] = u_ring
    x2 = jnp.where(ring_inside(), gain_u * u_ring + gain_s * operator_ring(), 0.0)
    ring_x2[...] = x2
    for p in range(4):
        for j in range(3):
            n = 3 + 3 * p + j
            main2[p, j] = x2[8 * n : 8 * n + 8, 0:128]
    pack_y(main2, ypack2, 3)
    zpack2[...] = pack_z(main2, ypack2, 3)
    z_second = send_z(zpack2, rz2)
    faces_second = send_faces(main2, ypack2, rx2, ry2)

    applied = operator_local(x2)
    even = (lane8 * 2) & 127

    def coarse_sum(source, n):
        value = source[n, pl.ds(0, 8, 2), :] + source[n, pl.ds(1, 8, 2), :]
        value = value + pltpu.roll(value, 127, 1)
        return jnp.take_along_axis(value, even, axis=1, mode="promise_in_bounds")

    for big in range(2):
        resid[3, 8 * big : 8 * big + 8, :] = eta[2 * big] + eta[2 * big + 1]
        for j in range(3):
            total = jnp.zeros((8, 128), F32)
            for p in (2 * big, 2 * big + 1):
                n = 3 * p + j
                total = total + eta[p] * (main[p, j] - applied[8 * n : 8 * n + 8, 0:128])
            resid[j, 8 * big : 8 * big + 8, :] = total
    four_over = 4.0 / coarse_sum(resid, 3)
    total = jnp.zeros((8, 128), F32)
    for j in range(3):
        value = coarse_sum(resid, j) * four_over
        cmain[j] = value
        first = (lane8 >= 64 + 4 * j) & (lane8 < 66 + 4 * j)
        last = ((lane8 + (130 - 4 * j)) & 127) < 2
        total = jnp.where(first | last, pltpu.roll(value, 64 + 4 * j, 1), total)
    czpack[...] = total
    z_coarse = send_z(czpack, rcz)
    main_coarse = send_sides(cmain, rc)

    store_wide(wide_p, 4, (3,), wide_p_code, main, rx, ry, zmerged, rf)
    q_ring = ring_of(wide_p, 1)
    high, low = split(wide_p[...])
    gap = jnp.zeros((32, 256), BF16)
    near = jnp.dot(face1[...], jnp.concatenate([high, gap, low, gap], axis=0), preferred_element_type=F32)
    near = near + pltpu.roll(q_ring, 1, 1) + pltpu.roll(q_ring, 255, 1)
    p_ring = (4.0 / 27.0) * q_ring + (1.0 / 81.0) * near
    p_ring = jnp.where(inside(code256[ring_p_code : ring_p_code + 64, :]), p_ring, 0.0)
    high, low = split(p_ring)
    near = jnp.dot(face2[...], jnp.concatenate([high, low], axis=0), preferred_element_type=F32)
    p_in, q_in = p_ring[8:40], q_ring[8:40]
    near = near + pltpu.roll(p_in, 1, 1) + pltpu.roll(p_in, 255, 1)
    p_out = (1.0 / 3.0) * p_in + (1.0 / 9.0) * q_in + (1.0 / 9.0) * near
    for p in range(4):
        pout_ref[p] = p_out[8 * p : 8 * p + 8, 0:128]

    for copy in z_second:
        copy.wait_recv()
    zmerged2[...] = merge_z(rz2)
    sides_second = send_sides(zmerged2, rf2)

    for copy in z_coarse:
        copy.wait_recv()
    czmerged[...] = jnp.where((lane8 >= 64) & (lane8 < 96), rcz[1], rcz[0])
    sides_coarse = send_sides(czmerged, rcf)

    for copy in faces_second:
        copy.wait_recv()
    for copy in sides_second:
        copy.wait_recv()
    store_wide(wide, 3, (0, 1, 2), 0, main2, rx2, ry2, zmerged2, rf2)
    ring_t[...] = operator_ring()

    for copy in main_coarse:
        copy.wait_recv()
    for copy in sides_coarse:
        copy.wait_recv()

    blocks = []
    n = 0
    for dx in (-1, 0, 1):
        for dy in (-1, 0, 1):
            for j in range(3):
                if (dx, dy) == (0, 0):
                    inner, merged = cmain[j], czmerged[...]
                else:
                    slot = side[(-dx, -dy)]
                    inner, merged = rc[slot, j], rcf[slot]
                value = jnp.where(lane8 < 64, inner, tile_edge(merged, j))
                blocks.append(jnp.where(inside(code128[8 * n : 8 * n + 8, :]), value, 0.0))
                n += 1
    blocks.append(jnp.zeros((40, 128), F32))
    high, low = split(jnp.concatenate(blocks, axis=0))
    base = w_base("coarse")
    product = jnp.dot(
        w[base : base + 320, :], jnp.concatenate([high, high, low], axis=0), preferred_element_type=F32
    )
    e = gain_u[:, 0:128] * product[240:320] + gain_s[:, 0:128] * z_shift_sum(product, 80)
    e = jnp.where(inside(code128[216:296, :]), e, 0.0)
    lane80 = lax.broadcasted_iota(jnp.int32, (80, 128), 1)
    near_lane = lane80 >> 1
    far_lane = jnp.where(lane80 < 2, 64, jnp.where(lane80 >= 126, 127, 100))
    e = jnp.concatenate(
        [
            jnp.take_along_axis(e, near_lane, axis=1, mode="promise_in_bounds"),
            jnp.take_along_axis(e, far_lane, axis=1, mode="promise_in_bounds"),
        ],
        axis=1,
    )
    high, low = split(e)
    gap = jnp.zeros((48, 256), BF16)
    right = jnp.concatenate([high, gap, high, gap, low, gap], axis=0)
    product = jnp.dot(w_fine[...], right, preferred_element_type=F32)
    moved = ring_u[...] - (ring_t[...] + z_shift_sum(product, 192))
    step = ((1.0 / THETA) * ikc) * moved
    x = jnp.where(ring_inside(), ring_x2[...] + product[576:768] + step, 0.0)
    applied = operator_local(x)
    final = (
        x[24:120] + MOM * step[24:120] + (WEIGHT * ikc) * (ring_u[24:120, :] - applied)
    )
    for p in range(4):
        for j in range(3):
            n = 3 * p + j
            out_ref[j, p] = final[8 * n : 8 * n + 8, 0:128]

    for copy in sent:
        copy.wait_send()


COPIES = 2 * (2 + 8 + 8) + 2 + 8 + 8


def scratch():
    vmem = pltpu.VMEM
    fine_rows = 4 * 192

    def exchange(comps):
        return [
            vmem((4, comps, 8, 128), F32),
            vmem((2, comps, 8, 128), F32),
            vmem((8, 128), F32),
            vmem((8, 128), F32),
            vmem((2, 2, comps, 8, 128), F32),
            vmem((2, 3, comps, 8, 128), F32),
            vmem((2, 8, 128), F32),
            vmem((8, 8, 128), F32),
        ]

    return [
        vmem((3, 4, 8, 128), F32),
        vmem((4, 8, 128), F32),
        vmem((4, 8, 128), jnp.int32),
        pltpu.SMEM((8,), F32),
        pltpu.SMEM((3, 3, 27), F32),
        vmem(INDEX.shape, jnp.int32),
        vmem(CODE_256.shape, jnp.int32),
        vmem(CODE_128.shape, jnp.int32),
        vmem(FACE_1.shape, BF16),
        vmem(FACE_2.shape, BF16),
        vmem((4, 8, 128), F32),
        *exchange(4),
        *exchange(3),
        vmem((3, 8, 128), F32),
        vmem((8, 128), F32),
        vmem((8, 128), F32),
        vmem((8, 3, 8, 128), F32),
        vmem((2, 8, 128), F32),
        vmem((8, 8, 128), F32),
        vmem((9, 16, 128), F32),
        vmem((W_ROWS - fine_rows, 768), BF16),
        vmem((fine_rows, 384), BF16),
        vmem((288, 256), F32),
        vmem((96, 256), F32),
        vmem((192, 256), F32),
        vmem((192, 256), F32),
        vmem((192, 256), F32),
        vmem((4, 16, 128), F32),
        vmem((8, 128), F32),
        pltpu.SemaphoreType.DMA((10,)),
        pltpu.SemaphoreType.DMA((COPIES,)),
        pltpu.SemaphoreType.DMA((COPIES,)),
    ]


def on_device(rhs_velocity, rhs_pressure, layer_ids, visc_table, stencil):
    anywhere = pl.BlockSpec(memory_space=pltpu.HBM)
    inside = pl.BlockSpec(memory_space=pltpu.VMEM)
    return pl.pallas_call(
        body,
        name="stokes",
        out_shape=(
            jax.ShapeDtypeStruct(rhs_velocity.shape, F32),
            jax.ShapeDtypeStruct(rhs_pressure.shape, F32),
        ),
        in_specs=[anywhere] * 10,
        out_specs=(inside, inside),
        scratch_shapes=scratch(),
        compiler_params=pltpu.CompilerParams(
            collective_id=0, has_side_effects=True, vmem_limit_bytes=60 * 1024 * 1024
        ),
    )(
        rhs_velocity,
        rhs_pressure,
        layer_ids,
        visc_table,
        stencil.transpose(1, 2, 0),
        jnp.asarray(INDEX),
        jnp.asarray(CODE_256),
        jnp.asarray(CODE_128),
        jnp.asarray(FACE_1, BF16),
        jnp.asarray(FACE_2, BF16),
    )


def solution(mesh):
    placed = (P(None, "gx", "gy", "gz"), P("gx", "gy", "gz"), P("gx", "gy", "gz"), P(), P())
    return jax.shard_map(
        on_device,
        mesh=mesh,
        in_specs=placed,
        out_specs=(P(None, "gx", "gy", "gz"), P("gx", "gy", "gz")),
        check_vma=False,
    )
```

profile of v0, /device:TPU:1, one launch (start us, length us, event | category | flops | bytes accessed | tf_op | source)
XLA Modules:
  0.0 45.6 jit_solution(10132942266404390231)
XLA Ops:
  0.6 42.9 %stokes.1 = (f32[3,4,8,128]{3,2,1,0:T(8,128)}, f32[4,8,128]{2,1,0:T(8,128)}) custom-call(f32[3,4,8,128]{3,2,1,0:T(8,128)} %rhs_hbm.1, f32[4,8,128]{2,1,0:T(8,128)} %press_hbm.1, s32[4,8,128]{2,1,0:T(8,128)} %ids_hbm.1, f32[8]{0:T(128)} %visc_hbm.1, f32[3,3,27]{2,1,0:T(4,128)} %bitcast.1, s32[896,256]{1,0:T(8,128)} %constant.10.clone.index_hbm, ...), custom_call_target="tpu_custom_call" | custom-call | tf_op jit(solution)/shard_map/stokes/pallas_call | solution.py:744
  43.5 0.0 copy-start
  43.5 1.4 %copy.14 = f32[3,4,8,128]{3,2,1,0:T(8,128)} copy(f32[3,4,8,128]{3,2,1,0:T(8,128)} %get-tuple-element.4) | data formatting | bytes 98304
  45.0 0.0 copy-done
  45.0 0.6 %copy.15 = f32[4,8,128]{2,1,0:T(8,128)} copy(f32[4,8,128]{2,1,0:T(8,128)S(1)} %copy-done) | data formatting | bytes 32768
Async XLA Ops:
  43.5 1.4 %copy-start = (f32[4,8,128]{2,1,0:T(8,128)S(1)}, f32[4,8,128]{2,1,0:T(8,128)}, u32[]{:S(2)}) copy-start(f32[4,8,128]{2,1,0:T(8,128)} %get-tuple-element.5) | copy-start | bytes 49156
where the time goes:
time: 45.8 us; the launch traced here: 45.6 us
  Pallas kernels  42.9 us (94%)
  local copies, waits for them, and re-layouts  2.04 us (4%)
  between operations  0.65 us (1%)
    pallas_call x1, Pallas kernels, on_device(): pl.pallas_call(body, name='stokes', out_shape=(jax.ShapeDtypeStruct(rhs_v...  42.9 us
    unnamed x4, local copies, waits for them, and re-layouts  2.04 us

commit v1 on v0

v1 whole, which is shorter than its diff:
```python
import functools

import numpy as np
import jax
import jax.numpy as jnp
from jax import lax
from jax.experimental import pallas as pl
from jax.experimental.pallas import tpu as pltpu
from jax.sharding import PartitionSpec as P

F32 = jnp.float32
BF16 = jnp.bfloat16
MESH = pl.DeviceIdType.MESH

THETA = (1.8 + 0.2) / 2.0
DELTA = (1.8 - 0.2) / 2.0
SIGMA = THETA / DELTA
RHO0 = 1.0 / SIGMA
RHO1 = 1.0 / (2.0 * SIGMA - RHO0)
MOM = RHO1 * RHO0
WEIGHT = 2.0 * RHO1 / DELTA

XLO, XHI, YLO, YHI, ZLO, ZHI, NEVER = 1, 2, 4, 8, 16, 32, 64

ONE, ZERO = 28, 31

CORNER_X = (4, 5, -2, -1)
SIDES = [(dx, dy) for dx in (-1, 0, 1) for dy in (-1, 0, 1) if (dx, dy) != (0, 0)]
AHEAD = [(dy, dz) for dy in (0, -1, 1) for dz in (-1, 1)]


def plane_block(x, j):
    return [(x, r, j) for r in range(8)]


def y_block(s, j):
    return [(r // 2, (-2 if s == 0 else 8) + r % 2, j) for r in range(8)]


def c_block(s, j):
    return [(CORNER_X[r // 2], (-2 if s == 0 else 8) + r % 2, j) for r in range(8)]


def edge_block(i, half):
    rows = []
    for r in range(8):
        y = -1 if r % 2 else 8
        if half == 0:
            x = r // 2 if r < 4 else (-1 if r >= 6 else None)
        else:
            x = r // 2 if r >= 4 else (4 if r < 2 else None)
        rows.append(None if x is None else (x, y, i))
    return rows


def rows_wide(comps):
    rows = []
    for x in (-2, -1, 0, 1, 2):
        for j in range(comps):
            rows += plane_block(x, j)
    for block in (y_block, c_block):
        for s in range(2):
            for j in range(comps):
                rows += block(s, j)
    for x in (3, 4, 5):
        for j in range(comps):
            rows += plane_block(x, j)
    return rows


def rows_half(half, comps):
    rows = []
    for x in ((-1, 0, 1), (2, 3, 4))[half]:
        for i in range(comps):
            rows += plane_block(x, i)
    for i in range(comps):
        rows += edge_block(i, half)
    return rows


def rows_ring(comps):
    return rows_half(0, comps) + rows_half(1, comps)


def rows_coarse_in():
    rows = []
    for dx in (-1, 0, 1):
        for j in range(3):
            rows += [(2 * dx + r // 4, r % 4, j) for r in range(8)]
        for j in range(3):
            rows += [(2 * dx + r // 4, r % 4 + (4 if r % 4 < 2 else -4), j) for r in range(8)]
    return rows


def rows_coarse_out():
    rows = []
    for q in range(3):
        for i in range(3):
            for r in range(8):
                n = 8 * q + r
                rows.append((n // 6 - 1, n % 6 - 1, i))
    return rows + [None] * 8


def index_stencil(outs, ins):
    table = np.full((len(outs), len(ins)), ZERO, np.int32)
    for m, out in enumerate(outs):
        if out is None:
            continue
        for k, source in enumerate(ins):
            if source is None:
                continue
            a, b = source[0] - out[0] + 1, source[1] - out[1] + 1
            if 0 <= a <= 2 and 0 <= b <= 2:
                table[m, k] = 3 * (3 * a + b) + source[2]
    return table


def index_same(outs, ins, scale):
    table = np.full((len(outs), len(ins)), ZERO, np.int32)
    for m, out in enumerate(outs):
        if out is None:
            continue
        for k, source in enumerate(ins):
            if source is not None and (out[0] // scale, out[1] // scale, out[2]) == source:
                table[m, k] = ONE
    return table


def index_refined(outs, ins):
    table = np.full((len(outs), len(ins)), ZERO, np.int32)
    for m, out in enumerate(outs):
        if out is None:
            continue
        for k, source in enumerate(ins):
            if source is None:
                continue
            a = [v for v in range(3) if (out[0] + v - 1) // 2 == source[0]]
            b = [v for v in range(3) if (out[1] + v - 1) // 2 == source[1]]
            if a and b:
                segment = (len(a) - 1) + 2 * (len(b) - 1)
                table[m, k] = 32 * segment + 3 * (3 * a[0] + b[0]) + source[2]
    return table


def codes(rows, x_end, y_end, lanes, z_bits):
    table = np.full((len(rows), lanes), NEVER, np.int32)
    z_row = np.full((lanes,), NEVER, np.int32)
    for lane, bits in z_bits:
        z_row[lane] = bits
    for m, row in enumerate(rows):
        if row is None:
            continue
        bits = (XLO if row[0] < 0 else 0) | (XHI if row[0] >= x_end else 0)
        bits |= (YLO if row[1] < 0 else 0) | (YHI if row[1] >= y_end else 0)
        table[m] = bits | z_row
    return table


def face_matrix(outs, ins):
    table = np.zeros((len(outs), len(ins)), np.float32)
    for m, out in enumerate(outs):
        if out is None:
            continue
        for k, source in enumerate(ins):
            if source is not None and abs(source[0] - out[0]) + abs(source[1] - out[1]) == 1:
                table[m, k] = 1.0
    return table


FINE_LANES = [(z, 0) for z in range(128)]
WIDE_Z = FINE_LANES + [(128, ZHI), (129, ZHI), (254, ZLO), (255, ZLO)]
RING_Z = FINE_LANES + [(128, ZHI), (255, ZLO)]
COARSE_Z = [(z, 0) for z in range(64)] + [(64, ZHI), (65, ZHI), (126, ZLO), (127, ZLO)]
COARSE_RING_Z = [(z, 0) for z in range(64)] + [(64, ZHI), (127, ZLO)]

WIDE = rows_wide(3)
RING = rows_ring(3)
LOCAL = [row for x in range(4) for i in range(3) for row in plane_block(x, i)]
HALF_A = rows_half(0, 3)
HALF_B = rows_half(1, 3)
COARSE_IN = rows_coarse_in()
COARSE_OUT = rows_coarse_out()

def triple(table, width):
    wide = np.full((len(table), width), ZERO, np.int32)
    count = table.shape[1]
    for n in range(3):
        wide[:, n * count : (n + 1) * count] = table
    return wide


def single(table):
    return np.concatenate([table, np.full((len(table), 256 - table.shape[1]), ZERO, np.int32)], axis=1)


def place(sections):
    places, at, row = {}, 0, 0
    for name, table, copies in sections:
        places[name] = (at, len(table), copies, row)
        at += len(table)
        row += len(table) * copies
    return places, np.concatenate([section[1] for section in sections], axis=0), row


WIDE_SECTIONS, WIDE_INDEX, WIDE_ROWS = place(
    [
        ("a", single(index_stencil(HALF_A, WIDE[0:256])), 3),
        ("b", single(index_stencil(HALF_B, WIDE[32:288])), 3),
        ("local", single(index_stencil(LOCAL, RING)), 3),
    ]
)
COARSE_SECTIONS, COARSE_INDEX, COARSE_ROWS = place(
    [
        ("coarse", triple(index_stencil(COARSE_OUT, COARSE_IN), 512), 3),
        ("keep", triple(index_same(COARSE_OUT, COARSE_IN, 1), 512), 1),
    ]
)
FINE_SECTIONS, FINE_INDEX, FINE_ROWS = place(
    [
        ("fine", triple(index_refined(RING, COARSE_OUT), 256), 3),
        ("spread", triple(index_same(RING, COARSE_OUT, 2), 256), 1),
    ]
)

CODE_WIDE = codes(WIDE, 4, 8, 256, WIDE_Z)
CODE_RING = codes(RING, 4, 8, 256, RING_Z)
CODE_COARSE = codes(COARSE_IN, 2, 4, 128, COARSE_Z)
CODE_COARSE_RING = codes(COARSE_OUT, 2, 4, 128, COARSE_RING_Z)
CODE_WIDE_P = codes(rows_wide(1), 4, 8, 256, WIDE_Z)
CODE_RING_P = codes(rows_ring(1), 4, 8, 256, RING_Z)
CODE_256 = np.concatenate([CODE_WIDE, CODE_RING, CODE_WIDE_P, CODE_RING_P], axis=0)
CODE_128 = np.concatenate([CODE_COARSE, CODE_COARSE_RING], axis=0)


def face_pair(outs, ins, width, total):
    single = face_matrix(outs, ins)
    table = np.zeros((len(outs), total), np.float32)
    table[:, : single.shape[1]] = single
    table[:, width : width + single.shape[1]] = single
    return table


FACE_1 = face_pair(rows_ring(1), rows_wide(1), 128, 256)
FACE_2 = face_pair([row for x in range(4) for row in plane_block(x, 0)], rows_ring(1), 64, 128)


def split(value):
    high = value.astype(BF16)
    low = (value - high.astype(F32)).astype(BF16)
    return high, low


def z_shift_sum(product, rows):
    lanes = product.shape[1]
    return (
        product[rows : 2 * rows]
        + pltpu.roll(product[0:rows], 1, 1)
        + pltpu.roll(product[2 * rows : 3 * rows], lanes - 1, 1)
    )


def body(
    rhs_hbm, press_hbm, ids_hbm, visc_hbm, stencil_hbm, windex_hbm, cindex_hbm, findex_hbm,
    code256_hbm, code128_hbm, face1_hbm, face2_hbm,
    out_ref, pout_ref,
    rhs, press, ids, visc, stencil, windex, cindex, findex, code256, code128, face1, face2,
    eta, main, ypack, zpack, zmerged, rx, ry, rz, rf,
    before, coarse, zpack2, zmerged2, rx2, rs2, rz2, rf2,
    tables, w, w_coarse, w_fine, wide, wide_p, ring_x, resid,
    in_sem, send_sem, recv_sem,
):
    nx, ny, nz = (lax.axis_size(name) for name in ("gx", "gy", "gz"))
    ix, iy, iz = (lax.axis_index(name) for name in ("gx", "gy", "gz"))
    ends = {
        ("x", -1): ix > 0, ("x", 1): ix < nx - 1,
        ("y", -1): iy > 0, ("y", 1): iy < ny - 1,
        ("z", -1): iz > 0, ("z", 1): iz < nz - 1,
    }

    def present(dx, dy, dz):
        found = None
        for axis, step in (("x", dx), ("y", dy), ("z", dz)):
            if step:
                one = ends[axis, step]
                found = one if found is None else jnp.logical_and(found, one)
        return found

    def device(dx, dy, dz):
        return (ix + dx, iy + dy, iz + dz)

    partners = [(0, dy, dz) for dy, dz in AHEAD] + [(dx, dy, 0) for dx, dy in SIDES]
    barrier = pltpu.get_barrier_semaphore()
    expected = 0
    for where in partners:
        there = present(*where)
        expected = expected + there.astype(jnp.int32)

        @pl.when(there)
        def _():
            pl.semaphore_signal(barrier, inc=1, device_id=device(*where), device_id_type=MESH)

    loads = [
        pltpu.make_async_copy(source, target, in_sem.at[n])
        for n, (source, target) in enumerate(
            [
                (visc_hbm, visc), (ids_hbm, ids), (rhs_hbm, rhs), (press_hbm, press), (stencil_hbm, stencil),
                (windex_hbm, windex), (code256_hbm, code256), (code128_hbm, code128),
                (cindex_hbm, cindex), (findex_hbm, findex), (face1_hbm, face1), (face2_hbm, face2),
            ]
        )
    ]
    for load in loads:
        load.start()

    counter = [0]
    sent = []

    def send(source, target, where):
        n = counter[0]
        counter[0] += 1
        copy = pltpu.make_async_remote_copy(
            src_ref=source,
            dst_ref=target,
            send_sem=send_sem.at[n],
            recv_sem=recv_sem.at[n],
            device_id=device(*where),
            device_id_type=MESH,
        )
        pl.when(present(*where))(copy.start)
        sent.append((copy, present(*where)))
        return copy, present(*(-step for step in where))

    def receive(copies):
        for copy, there in copies:
            pl.when(there)(copy.wait_recv)

    bad = NEVER
    for bit, end in (
        (XLO, ("x", -1)), (XHI, ("x", 1)), (YLO, ("y", -1)), (YHI, ("y", 1)), (ZLO, ("z", -1)), (ZHI, ("z", 1)),
    ):
        bad = bad + bit * (1 - ends[end].astype(jnp.int32))

    lane8 = lax.broadcasted_iota(jnp.int32, (8, 128), 1)
    row8 = lax.broadcasted_iota(jnp.int32, (8, 128), 0)
    low_rows = row8 < 4
    odd_rows = (row8 & 1) == 1

    def inside(code):
        return (code & bad) == 0

    def roll(value, shift):
        return pltpu.roll(value, shift % 128, 1) if shift % 128 else value

    for load in loads[:4]:
        load.wait()
    for p in range(4):
        layer = ids[p]
        value = jnp.zeros((8, 128), F32)
        for k in range(8):
            value = value + jnp.where(layer == k, visc[k], 0.0)
        eta[p] = value
        inverse = 1.0 / value
        for j in range(3):
            main[p, j] = rhs[j, p] * inverse
        main[p, 3] = press[p] * value

    for s in range(2):
        for j in range(4):
            for p in range(4):
                ypack[s, j, 2 * p : 2 * p + 2, :] = main[p, j, 6 * s : 6 * s + 2, :]
    items = [main[p, j] for p in range(4) for j in range(4)] + [ypack[s, j] for s in range(2) for j in range(4)]
    total = jnp.zeros((8, 128), F32)
    for k, value in enumerate(items):
        total = jnp.where(((lane8 + (130 - 4 * k)) & 127) < 4, roll(value, 4 * k), total)
    zpack[...] = total

    pl.semaphore_wait(barrier, expected)

    def send_ahead(source, slots):
        return [send(source, slots.at[0 if dz > 0 else 1, 1 - dy], (0, dy, dz)) for dy, dz in AHEAD]

    def send_on(source, slots):
        return [send(source, slots.at[0 if dx > 0 else 1], (dx, 0, 0)) for dx in (-1, 1)]

    ahead_first = send_ahead(zpack, rz)
    faces_first = []
    for dx in (-1, 1):
        planes = main.at[pl.ds(0 if dx < 0 else 2, 2)]
        faces_first.append(send(planes, rx.at[0 if dx > 0 else 1], (dx, 0, 0)))
    for dy in (-1, 1):
        for dx in (0, -1, 1):
            faces_first.append(
                send(ypack.at[0 if dy < 0 else 1], ry.at[0 if dy > 0 else 1, 1 - dx], (dx, dy, 0))
            )

    loads[4].wait()
    kc = (stencil[0, 0, 13] + stencil[1, 1, 13] + stencil[2, 2, 13]) / 3.0
    for c in range(3):
        rows = []
        for i in range(3):
            base = jnp.zeros((8, 128), F32)
            for a in range(3):
                for b in range(3):
                    for j in range(3):
                        at = 3 * (3 * a + b) + j
                        base = jnp.where(lane8 == at, stencil[i, j, 9 * a + 3 * b + c], base)
            low = lane8 < 27
            pair_a = base + jnp.where(low, roll(base, -9), 0.0)
            pair_b = base + jnp.where(low, roll(base, -3), 0.0)
            pair_ab = pair_a + jnp.where(low, roll(pair_a, -3), 0.0)
            full = base + roll(pair_a, 32) + roll(pair_b, 64) + roll(pair_ab, 96)
            rows.append(jnp.where(lane8 == ONE, 1.0, full))
        for combo, (one, two) in enumerate(((0, 1), (2, 0), (1, 2))):
            tables[3 * c + combo, 0:8, :] = rows[one]
            tables[3 * c + combo, 8:16, :] = rows[two]

    lane16 = lax.broadcasted_iota(jnp.int32, (16, 128), 1)

    def build(index, section, target, tiles, width, unroll):
        at, count, copies, first = section

        def chunk(t):
            combo = lax.rem(t, 3)
            start = pl.multiple_of(t * 16, 16)
            for tile in range(tiles):
                lanes = slice(128 * tile, 128 * tile + 128)
                picked = index[pl.ds(at + start, 16), lanes]
                for c in range(copies):
                    value = jnp.take_along_axis(
                        tables[3 * c + combo], picked, axis=1, mode="promise_in_bounds"
                    )
                    rows = pl.ds(first + c * count + start, 16)
                    if width is None:
                        high, low = split(value)
                        target[rows, lanes] = high
                        target[rows, 256 + 128 * tile : 384 + 128 * tile] = low
                        target[rows, 512 + 128 * tile : 640 + 128 * tile] = high
                    else:
                        low = value - value.astype(BF16).astype(F32)
                        lane = lane16 + 128 * tile
                        value = jnp.where((lane >= width) & (lane < 2 * width), low, value)
                        target[rows, lanes] = value.astype(BF16)

        def step(t, carry):
            for n in range(unroll):
                chunk(t * unroll + n)
            return carry

        lax.fori_loop(0, count // (16 * unroll), step, 0)

    loads[5].wait()
    for name in ("a", "b", "local"):
        build(windex, WIDE_SECTIONS[name], w, 2, None, 3)
    for load in loads[6:]:
        load.wait()

    receive(ahead_first)
    for n in range(3):
        zmerged[n] = jnp.where((lane8 & 3) < 2, rz[1, n], rz[0, n])
    on_first = send_on(zmerged, rf)

    def along_z(own, passed, ox, oy):
        return own[oy + 1] if ox == 0 else passed[0 if ox < 0 else 1, oy + 1]

    def wide_blocks(comp, tile):
        comps = 4

        def edge(ox, oy, k):
            return roll(along_z(zmerged, rf, ox, oy), -4 * k)

        blocks = {}
        for p in range(4):
            blocks[p] = edge(0, 0, p * comps + comp) if tile else main[p, comp]
        for n in range(2):
            blocks[n - 2] = edge(-1, 0, (n + 2) * comps + comp) if tile else rx[0, n, comp]
            blocks[n + 4] = edge(1, 0, n * comps + comp) if tile else rx[1, n, comp]
        for s, oy in enumerate((-1, 1)):
            k = 4 * comps + (1 - s) * comps + comp
            level, above, below = (edge(ox, oy, k) if tile else ry[s, ox + 1, comp] for ox in (0, 1, -1))
            blocks["y", s] = level
            blocks["c", s] = jnp.where(low_rows, above, below)
        return blocks

    def store_wide(target, comps, code_at, tile):
        lanes = slice(128 * tile, 128 * tile + 128)
        for slot, comp in enumerate(comps):
            blocks = wide_blocks(comp, tile)
            order = [-2, -1, 0, 1, 2, ("y", 0), ("y", 1), ("c", 0), ("c", 1), 3, 4, 5]
            for n, key in enumerate(order):
                at = 8 * (n * len(comps) + slot)
                code = code256[code_at + at : code_at + at + 8, lanes]
                target[at : at + 8, lanes] = jnp.where(inside(code), blocks[key], 0.0)

    def ring_of(source, comps):
        def block(n):
            return source[8 * comps * n : 8 * comps * (n + 1), :]

        row = lax.broadcasted_iota(jnp.int32, (8 * comps, 256), 0)
        odd, low = (row & 1) == 1, (row & 7) < 4
        level = jnp.where(odd, block(5), block(6))
        corner = jnp.where(odd, block(7), block(8))
        return jnp.concatenate(
            [
                block(1), block(2), block(3), jnp.where(low, level, corner),
                block(4), block(9), block(10), jnp.where(low, corner, level),
            ],
            axis=0,
        )

    def local_of(ring, comps):
        return jnp.concatenate([ring[8 * comps : 24 * comps], ring[32 * comps : 48 * comps]], axis=0)

    def operator_ring():
        parts = []
        for name, start in (("a", 0), ("b", 32)):
            high, low = split(wide[start : start + 256, :])
            right = jnp.concatenate([high, high, low], axis=0)
            base = WIDE_SECTIONS[name][3]
            product = jnp.dot(w[base : base + 288, :], right, preferred_element_type=F32)
            parts.append(z_shift_sum(product, 96))
        return jnp.concatenate(parts, axis=0)

    def operator_local(value):
        high, low = split(value)
        gap = jnp.zeros((64, 256), BF16)
        right = jnp.concatenate([high, gap, high, gap, low, gap], axis=0)
        base = WIDE_SECTIONS["local"][3]
        product = jnp.dot(w[base : base + 288, :], right, preferred_element_type=F32)
        return z_shift_sum(product, 96)

    ikc = (jnp.full((8, 256), 1.0, F32) / kc)[0:1, :]
    gain_u = ((1.0 + MOM + WEIGHT * THETA) / THETA) * ikc
    gain_s = (-WEIGHT / THETA) * ikc * ikc

    ring_code = len(CODE_WIDE)
    wide_p_code = ring_code + len(CODE_RING)
    ring_p_code = wide_p_code + len(CODE_WIDE_P)

    def ring_inside():
        return inside(code256[ring_code : ring_code + 192, :])

    receive(faces_first)
    store_wide(wide, (0, 1, 2), 0, 0)
    receive(on_first)

    store_wide(wide, (0, 1, 2), 0, 1)
    x2 = jnp.where(ring_inside(), gain_u * ring_of(wide, 3) + gain_s * operator_ring(), 0.0)
    ring_x[...] = x2

    applied = operator_local(x2)
    even = (lane8 * 2) & 127

    def coarse_sum(source, n):
        value = source[n, pl.ds(0, 8, 2), :] + source[n, pl.ds(1, 8, 2), :]
        value = value + roll(value, -1)
        return jnp.take_along_axis(value, even, axis=1, mode="promise_in_bounds")

    def local_row(p):
        return 8 * (3 + 3 * p if p < 2 else 6 + 3 * p)

    for big in range(2):
        resid[3, 8 * big : 8 * big + 8, :] = eta[2 * big] + eta[2 * big + 1]
        for j in range(3):
            total = jnp.zeros((8, 128), F32)
            for p in (2 * big, 2 * big + 1):
                n = 8 * (3 * p + j)
                left = main[p, j] - applied[n : n + 8, 0:128]
                resid[4 + j, 8 * p : 8 * p + 8, :] = left
                at = local_row(p) + 8 * j
                value = ring_x[at : at + 8, 0:128] + ((1.0 / THETA) * ikc[:, 0:128]) * left
                before[p, j] = value
                total = total + eta[p] * left
            resid[j, 8 * big : 8 * big + 8, :] = total
    four_over = 4.0 / coarse_sum(resid, 3)
    total = jnp.zeros((8, 128), F32)
    for j in range(3):
        value = coarse_sum(resid, j) * four_over
        coarse[j] = value
        first = (lane8 >= 98 + 4 * j) & (lane8 < 100 + 4 * j)
        last = (lane8 >= 32 + 4 * j) & (lane8 < 34 + 4 * j)
        total = jnp.where(first | last, roll(value, 98 + 4 * j), total)
        for p in range(4):
            coarse[3 + j, 2 * p : 2 * p + 1, :] = before[p, j, 0:1, :]
            coarse[3 + j, 2 * p + 1 : 2 * p + 2, :] = before[p, j, 7:8, :]
    items = [before[p, j] for p in range(4) for j in range(3)] + [coarse[3 + j] for j in range(3)]
    for k, value in enumerate(items):
        total = jnp.where(((lane8 + (129 - 2 * k)) & 127) < 2, roll(value, 2 * k), total)
    zpack2[...] = total
    ahead_second = send_ahead(zpack2, rz2)
    side = {offset: n for n, offset in enumerate(SIDES)}
    sides_second = [
        send(coarse, rs2.at[side[(-dx, -dy)]], (dx, dy, 0)) for dx, dy in SIDES
    ]
    for dx in (-1, 1):
        sides_second.append(send(before.at[0 if dx < 0 else 3], rx2.at[0 if dx > 0 else 1], (dx, 0, 0)))

    store_wide(wide_p, (3,), wide_p_code, 0)
    store_wide(wide_p, (3,), wide_p_code, 1)
    q_ring = ring_of(wide_p, 1)
    high, low = split(wide_p[...])
    gap = jnp.zeros((32, 256), BF16)
    near = jnp.dot(face1[...], jnp.concatenate([high, gap, low, gap], axis=0), preferred_element_type=F32)
    near = near + pltpu.roll(q_ring, 1, 1) + pltpu.roll(q_ring, 255, 1)
    p_ring = (4.0 / 27.0) * q_ring + (1.0 / 81.0) * near
    p_ring = jnp.where(inside(code256[ring_p_code : ring_p_code + 64, :]), p_ring, 0.0)
    high, low = split(p_ring)
    near = jnp.dot(face2[...], jnp.concatenate([high, low], axis=0), preferred_element_type=F32)
    p_in, q_in = local_of(p_ring, 1), local_of(q_ring, 1)
    near = near + pltpu.roll(p_in, 1, 1) + pltpu.roll(p_in, 255, 1)
    p_out = (1.0 / 3.0) * p_in + (1.0 / 9.0) * q_in + (1.0 / 9.0) * near
    for p in range(4):
        pout_ref[p] = p_out[8 * p : 8 * p + 8, 0:128]
    for name in ("coarse", "keep"):
        build(cindex, COARSE_SECTIONS[name], w_coarse, 4, 144, 1)

    receive(ahead_second)
    from_high = ((lane8 < 32) & ((lane8 & 1) == 0)) | ((lane8 >= 64) & (lane8 < 127))
    for n in range(3):
        zmerged2[n] = jnp.where(from_high, rz2[1, n], rz2[0, n])
    on_second = send_on(zmerged2, rf2)

    for name in ("fine", "spread"):
        build(findex, FINE_SECTIONS[name], w_fine, 2, 80, 3)

    receive(sides_second)
    receive(on_second)

    def coarse_block(ox, oy, j):
        inner = coarse[j] if (ox, oy) == (0, 0) else rs2[side[(ox, oy)], j]
        return jnp.where(lane8 < 64, inner, roll(along_z(zmerged2, rf2, ox, oy), -(34 + 4 * j)))

    blocks = []
    near_high = (row8 & 3) < 2
    for ox in (-1, 0, 1):
        blocks += [coarse_block(ox, 0, j) for j in range(3)]
        blocks += [jnp.where(near_high, coarse_block(ox, 1, j), coarse_block(ox, -1, j)) for j in range(3)]
    value = jnp.where(inside(code128[0:144, :]), jnp.concatenate(blocks, axis=0), 0.0)
    high, low = split(value)
    right = jnp.concatenate([high, high, low, jnp.zeros((80, 128), BF16)], axis=0)
    product = jnp.dot(w_coarse[...], right, preferred_element_type=F32)
    e = gain_u[:, 0:128] * product[240:320] + gain_s[:, 0:128] * z_shift_sum(product, 80)
    e = jnp.where(inside(code128[144:224, :]), e, 0.0)
    lane80 = lax.broadcasted_iota(jnp.int32, (80, 128), 1)
    near_lane = lane80 >> 1
    far_lane = jnp.where(lane80 < 2, 64, jnp.where(lane80 >= 126, 127, 100))
    e = jnp.concatenate(
        [
            jnp.take_along_axis(e, near_lane, axis=1, mode="promise_in_bounds"),
            jnp.take_along_axis(e, far_lane, axis=1, mode="promise_in_bounds"),
        ],
        axis=1,
    )
    high, low = split(e)
    right = jnp.concatenate([high, high, low, jnp.zeros((16, 256), BF16)], axis=0)
    product = jnp.dot(w_fine[...], right, preferred_element_type=F32)

    def ring_block(ox, oy, inner, k):
        return jnp.concatenate([inner, roll(along_z(zmerged2, rf2, ox, oy), -2 * k)], axis=1)

    def layer(ox, oy, j):
        return ring_block(ox, oy, rs2[side[(ox, oy)], 3 + j], 12 + j)

    low_wide = lax.broadcasted_iota(jnp.int32, (8, 256), 0) < 4
    odd_wide = (lax.broadcasted_iota(jnp.int32, (8, 256), 0) & 1) == 1
    halves = [[], []]
    for half in range(2):
        for x in ((-1, 0, 1), (2, 3, 4))[half]:
            for j in range(3):
                if x == -1:
                    halves[half].append(ring_block(-1, 0, rx2[0, j], 9 + j))
                elif x == 4:
                    halves[half].append(ring_block(1, 0, rx2[1, j], j))
                else:
                    halves[half].append(ring_block(0, 0, before[x, j], 3 * x + j))
    for j in range(3):
        level = jnp.where(odd_wide, layer(0, -1, j), layer(0, 1, j))
        low_x = jnp.where(odd_wide, layer(-1, -1, j), layer(-1, 1, j))
        high_x = jnp.where(odd_wide, layer(1, -1, j), layer(1, 1, j))
        halves[0].append(jnp.where(low_wide, level, low_x))
        halves[1].append(jnp.where(low_wide, high_x, level))
    start = jnp.concatenate(halves[0] + halves[1], axis=0)

    down = ((1.0 / THETA) * ikc) * z_shift_sum(product, 192)
    x = jnp.where(ring_inside(), start + product[576:768] - down, 0.0)
    applied = operator_local(x)
    x_in, down_in = local_of(x, 3), local_of(down, 3)
    for p in range(4):
        for j in range(3):
            n = 8 * (3 * p + j)
            step = ((1.0 / THETA) * ikc[:, 0:128]) * resid[4 + j, 8 * p : 8 * p + 8, :] - down_in[n : n + 8, 0:128]
            out_ref[j, p] = (
                x_in[n : n + 8, 0:128]
                + MOM * step
                + (WEIGHT * ikc[:, 0:128]) * (main[p, j] - applied[n : n + 8, 0:128])
            )

    for copy, there in sent:
        pl.when(there)(copy.wait_send)


COPIES = 6 + 8 + 2 + 6 + 10 + 2


def scratch():
    vmem = pltpu.VMEM
    return [
        vmem((3, 4, 8, 128), F32),
        vmem((4, 8, 128), F32),
        vmem((4, 8, 128), jnp.int32),
        pltpu.SMEM((8,), F32),
        pltpu.SMEM((3, 3, 27), F32),
        vmem(WIDE_INDEX.shape, jnp.int32),
        vmem(COARSE_INDEX.shape, jnp.int32),
        vmem(FINE_INDEX.shape, jnp.int32),
        vmem(CODE_256.shape, jnp.int32),
        vmem(CODE_128.shape, jnp.int32),
        vmem(FACE_1.shape, BF16),
        vmem(FACE_2.shape, BF16),
        vmem((4, 8, 128), F32),
        vmem((4, 4, 8, 128), F32),
        vmem((2, 4, 8, 128), F32),
        vmem((8, 128), F32),
        vmem((3, 8, 128), F32),
        vmem((2, 2, 4, 8, 128), F32),
        vmem((2, 3, 4, 8, 128), F32),
        vmem((2, 3, 8, 128), F32),
        vmem((2, 3, 8, 128), F32),
        vmem((4, 3, 8, 128), F32),
        vmem((6, 8, 128), F32),
        vmem((8, 128), F32),
        vmem((3, 8, 128), F32),
        vmem((2, 3, 8, 128), F32),
        vmem((8, 6, 8, 128), F32),
        vmem((2, 3, 8, 128), F32),
        vmem((2, 3, 8, 128), F32),
        vmem((9, 16, 128), F32),
        vmem((WIDE_ROWS, 768), BF16),
        vmem((COARSE_ROWS, 512), BF16),
        vmem((FINE_ROWS, 256), BF16),
        vmem((288, 256), F32),
        vmem((96, 256), F32),
        vmem((192, 256), F32),
        vmem((7, 32, 128), F32),
        pltpu.SemaphoreType.DMA((12,)),
        pltpu.SemaphoreType.DMA((COPIES,)),
        pltpu.SemaphoreType.DMA((COPIES,)),
    ]


def on_device(rhs_velocity, rhs_pressure, layer_ids, visc_table, stencil):
    anywhere = pl.BlockSpec(memory_space=pltpu.HBM)
    inside = pl.BlockSpec(memory_space=pltpu.VMEM)
    return pl.pallas_call(
        body,
        name="stokes",
        out_shape=(
            pltpu.VMEM(rhs_velocity.shape, F32),
            pltpu.VMEM(rhs_pressure.shape, F32),
        ),
        in_specs=[anywhere] * 12,
        out_specs=(inside, inside),
        scratch_shapes=scratch(),
        compiler_params=pltpu.CompilerParams(
            collective_id=0, has_side_effects=True, vmem_limit_bytes=60 * 1024 * 1024
        ),
    )(
        *(
            pltpu.with_memory_space_constraint(value, pltpu.HBM)
            for value in (
                rhs_velocity,
                rhs_pressure,
                layer_ids,
                visc_table,
                stencil.transpose(1, 2, 0),
                jnp.asarray(WIDE_INDEX),
                jnp.asarray(COARSE_INDEX),
                jnp.asarray(FINE_INDEX),
                jnp.asarray(CODE_256),
                jnp.asarray(CODE_128),
                jnp.asarray(FACE_1, BF16),
                jnp.asarray(FACE_2, BF16),
            )
        )
    )


def solution(mesh):
    placed = (P(None, "gx", "gy", "gz"), P("gx", "gy", "gz"), P("gx", "gy", "gz"), P(), P())
    return jax.shard_map(
        on_device,
        mesh=mesh,
        in_specs=placed,
        out_specs=(P(None, "gx", "gy", "gz"), P("gx", "gy", "gz")),
        check_vma=False,
    )
```

time: 45.8 us -> 32.2 us (0.70)
  Pallas kernels: 42.9 us -> 30.2 us
  local copies, waits for them, and re-layouts: 2.04 us -> 1.23 us
    pallas_call x1, Pallas kernels: 42.9 us -> 30.2 us  [on_device(): pl.pallas_call(body, name='stokes', out_shape=(pltpu.VMEM(rhs_velocity.sh...]
    unnamed x4 -> x2, local copies, waits for them, and re-layouts: 2.04 us -> 1.23 us
where the time goes in v1:
time: 32.2 us; the launch traced here: 32.1 us
  Pallas kernels  30.2 us (94%)
  local copies, waits for them, and re-layouts  1.23 us (4%)
  between operations  0.64 us (2%)
    pallas_call x1, Pallas kernels, on_device(): pl.pallas_call(body, name='stokes', out_shape=(pltpu.VMEM(rhs_velocity.sh...  30.2 us
    unnamed x2, local copies, waits for them, and re-layouts  1.23 us

profile of v1, /device:TPU:1, one launch (start us, length us, event | category | flops | bytes accessed | tf_op | source)
XLA Modules:
  0.0 32.1 jit_solution(16816553512904167380)
XLA Ops:
  0.6 30.2 %stokes.1 = (f32[3,4,8,128]{3,2,1,0:T(8,128)S(1)}, f32[4,8,128]{2,1,0:T(8,128)S(1)}) custom-call(f32[3,4,8,128]{3,2,1,0:T(8,128)} %rhs_hbm.1, f32[4,8,128]{2,1,0:T(8,128)} %press_hbm.1, s32[4,8,128]{2,1,0:T(8,128)} %ids_hbm.1, f32[8]{0:T(128)} %visc_hbm.1, f32[3,3,27]{2,1,0:T(4,128)} %bitcast.1, s32[288,256]{1,0:T(8,128)} %constant.14.clone.windex_hbm, ...), custom_call_target="tpu_custom_call" | custom-call | tf_op jit(solution)/shard_map/stokes/pallas_call | solution.py:754
  30.8 0.6 %copy.16 = f32[3,4,8,128]{3,2,1,0:T(8,128)} copy(f32[3,4,8,128]{3,2,1,0:T(8,128)S(1)} %get-tuple-element.2) | data formatting | bytes 98304
  31.5 0.6 %copy.17 = f32[4,8,128]{2,1,0:T(8,128)} copy(f32[4,8,128]{2,1,0:T(8,128)S(1)} %get-tuple-element.3) | data formatting | bytes 32768

commit v2 on v1

--- a/solution.py
+++ b/solution.py
@@ -26,7 +26,7 @@
 
 CORNER_X = (4, 5, -2, -1)
 SIDES = [(dx, dy) for dx in (-1, 0, 1) for dy in (-1, 0, 1) if (dx, dy) != (0, 0)]
-AHEAD = [(dy, dz) for dy in (0, -1, 1) for dz in (-1, 1)]
+AHEAD = [(dx, dy, dz) for dx in (-1, 1, 0) for dy in (0, -1, 1) for dz in (-1, 1)]
 
 
 def plane_block(x, j):
@@ -265,9 +265,9 @@
     code256_hbm, code128_hbm, face1_hbm, face2_hbm,
     out_ref, pout_ref,
     rhs, press, ids, visc, stencil, windex, cindex, findex, code256, code128, face1, face2,
-    eta, main, ypack, zpack, zmerged, rx, ry, rz, rf,
-    before, coarse, zpack2, zmerged2, rx2, rs2, rz2, rf2,
-    tables, w, w_coarse, w_fine, wide, wide_p, ring_x, resid,
+    eta, main, qmain, ypack, qpack, cpack, zpack, rx, ry, rc, rqx, rqy, rz,
+    before, coarse, zpack2, xsend, ysend, csend, rx2, ry2, rc2, rz2,
+    tables, w, w_coarse, w_fine, wide, wide_p, ring_x, resid, blank,
     in_sem, send_sem, recv_sem,
 ):
     nx, ny, nz = (lax.axis_size(name) for name in ("gx", "gy", "gz"))
@@ -289,7 +289,7 @@
     def device(dx, dy, dz):
         return (ix + dx, iy + dy, iz + dz)
 
-    partners = [(0, dy, dz) for dy, dz in AHEAD] + [(dx, dy, 0) for dx, dy in SIDES]
+    partners = AHEAD + [(dx, dy, 0) for dx, dy in SIDES]
     barrier = pltpu.get_barrier_semaphore()
     expected = 0
     for where in partners:
@@ -300,40 +300,83 @@
         def _():
             pl.semaphore_signal(barrier, inc=1, device_id=device(*where), device_id_type=MESH)
 
-    loads = [
-        pltpu.make_async_copy(source, target, in_sem.at[n])
+    def load(n, pairs):
+        for source, target in pairs:
+            pltpu.make_async_copy(source, target, in_sem.at[n]).start()
+
+    def tiles(count):
+        return blank.at[pl.ds(0, count)]
+
+    def loaded(n, count):
+        pltpu.make_async_copy(tiles(count), tiles(count), in_sem.at[n]).wait()
+
+    visc_load = pltpu.make_async_copy(visc_hbm, visc, in_sem.at[0])
+    visc_load.start()
+    load(1, [(ids_hbm, ids), (rhs_hbm, rhs), (press_hbm, press)])
+    stencil_load = pltpu.make_async_copy(stencil_hbm, stencil, in_sem.at[2])
+    stencil_load.start()
+    windex_load = pltpu.make_async_copy(windex_hbm, windex, in_sem.at[3])
+    windex_load.start()
+    rest = [
+        pltpu.make_async_copy(source, target, in_sem.at[4 + n])
         for n, (source, target) in enumerate(
             [
-                (visc_hbm, visc), (ids_hbm, ids), (rhs_hbm, rhs), (press_hbm, press), (stencil_hbm, stencil),
-                (windex_hbm, windex), (code256_hbm, code256), (code128_hbm, code128),
-                (cindex_hbm, cindex), (findex_hbm, findex), (face1_hbm, face1), (face2_hbm, face2),
+                (code256_hbm, code256), (code128_hbm, code128), (cindex_hbm, cindex), (findex_hbm, findex),
+                (face1_hbm, face1), (face2_hbm, face2),
             ]
         )
     ]
-    for load in loads:
-        load.start()
-
-    counter = [0]
-    sent = []
-
-    def send(source, target, where):
-        n = counter[0]
-        counter[0] += 1
+    for copy in rest:
+        copy.start()
+
+    groups = []
+
+    def send(group, source, target, where):
         copy = pltpu.make_async_remote_copy(
             src_ref=source,
             dst_ref=target,
-            send_sem=send_sem.at[n],
-            recv_sem=recv_sem.at[n],
+            send_sem=send_sem.at[group],
+            recv_sem=recv_sem.at[group],
             device_id=device(*where),
             device_id_type=MESH,
         )
         pl.when(present(*where))(copy.start)
-        sent.append((copy, present(*where)))
-        return copy, present(*(-step for step in where))
-
-    def receive(copies):
-        for copy, there in copies:
-            pl.when(there)(copy.wait_recv)
+
+    count_x, count_y, count_z = (
+        ends[axis, -1].astype(jnp.int32) + ends[axis, 1].astype(jnp.int32) for axis in "xyz"
+    )
+
+    def wait_group(semaphore, choices):
+        for there, count in choices:
+
+            @pl.when(there)
+            def _():
+                pltpu.make_async_copy(tiles(count), tiles(count), semaphore).wait()
+
+    def plane_choices(corner, along_x, along_y):
+        return [
+            (
+                jnp.logical_and(count_x == nx, count_y == ny),
+                corner * nx * ny + along_x * nx + along_y * ny,
+            )
+            for nx in (1, 2)
+            for ny in (1, 2)
+        ]
+
+    def ahead_choices():
+        return [
+            (
+                jnp.logical_and(jnp.logical_and(count_x == nx, count_y == ny), count_z == nz),
+                (nx + 1) * (ny + 1) * nz,
+            )
+            for nx in (1, 2)
+            for ny in (1, 2)
+            for nz in (1, 2)
+        ]
+
+    def receive(group, choices):
+        wait_group(recv_sem.at[group], choices)
+        groups.append((group, choices))
 
     bad = NEVER
     for bit, end in (
@@ -352,8 +395,8 @@
     def roll(value, shift):
         return pltpu.roll(value, shift % 128, 1) if shift % 128 else value
 
-    for load in loads[:4]:
-        load.wait()
+    visc_load.wait()
+    loaded(1, 20)
     for p in range(4):
         layer = ids[p]
         value = jnp.zeros((8, 128), F32)
@@ -363,13 +406,23 @@
         inverse = 1.0 / value
         for j in range(3):
             main[p, j] = rhs[j, p] * inverse
-        main[p, 3] = press[p] * value
+        qmain[p] = press[p] * value
 
     for s in range(2):
-        for j in range(4):
-            for p in range(4):
+        for p in range(4):
+            for j in range(3):
                 ypack[s, j, 2 * p : 2 * p + 2, :] = main[p, j, 6 * s : 6 * s + 2, :]
-    items = [main[p, j] for p in range(4) for j in range(4)] + [ypack[s, j] for s in range(2) for j in range(4)]
+            qpack[s, 2 * p : 2 * p + 2, :] = qmain[p, 6 * s : 6 * s + 2, :]
+    for s in range(2):
+        for v, (one, two) in enumerate(((ypack[s, 0], ypack[s, 1]), (ypack[s, 2], qpack[s]))):
+            two = pltpu.roll(two, 4, 0)
+            cpack[0, s, v] = jnp.where(low_rows, one, two)
+            cpack[1, s, v] = jnp.where(low_rows, two, one)
+    items = []
+    for p in range(4):
+        items += [main[p, j] for j in range(3)] + [qmain[p]]
+    for s in range(2):
+        items += [ypack[s, j] for j in range(3)] + [qpack[s]]
     total = jnp.zeros((8, 128), F32)
     for k, value in enumerate(items):
         total = jnp.where(((lane8 + (130 - 4 * k)) & 127) < 4, roll(value, 4 * k), total)
@@ -377,24 +430,30 @@
 
     pl.semaphore_wait(barrier, expected)
 
-    def send_ahead(source, slots):
-        return [send(source, slots.at[0 if dz > 0 else 1, 1 - dy], (0, dy, dz)) for dy, dz in AHEAD]
-
-    def send_on(source, slots):
-        return [send(source, slots.at[0 if dx > 0 else 1], (dx, 0, 0)) for dx in (-1, 1)]
-
-    ahead_first = send_ahead(zpack, rz)
-    faces_first = []
+    def send_ahead(group, source, slots):
+        for dx, dy, dz in AHEAD:
+            send(group, source, slots.at[0 if dz > 0 else 1, 1 - dx, 1 - dy], (dx, dy, dz))
+
+    send_ahead(0, zpack, rz)
     for dx in (-1, 1):
-        planes = main.at[pl.ds(0 if dx < 0 else 2, 2)]
-        faces_first.append(send(planes, rx.at[0 if dx > 0 else 1], (dx, 0, 0)))
+        for dy in (-1, 1):
+            send(
+                1,
+                cpack.at[0 if dx < 0 else 1, 0 if dy < 0 else 1],
+                rc.at[0 if dx > 0 else 1, 0 if dy > 0 else 1],
+                (dx, dy, 0),
+            )
+        planes = pl.ds(0 if dx < 0 else 2, 2)
+        send(1, main.at[planes], rx.at[0 if dx > 0 else 1], (dx, 0, 0))
     for dy in (-1, 1):
-        for dx in (0, -1, 1):
-            faces_first.append(
-                send(ypack.at[0 if dy < 0 else 1], ry.at[0 if dy > 0 else 1, 1 - dx], (dx, dy, 0))
-            )
-
-    loads[4].wait()
+        send(1, ypack.at[0 if dy < 0 else 1], ry.at[0 if dy > 0 else 1], (0, dy, 0))
+    for dx in (-1, 1):
+        planes = pl.ds(0 if dx < 0 else 2, 2)
+        send(2, qmain.at[planes], rqx.at[0 if dx > 0 else 1], (dx, 0, 0))
+    for dy in (-1, 1):
+        send(2, qpack.at[0 if dy < 0 else 1], rqy.at[0 if dy > 0 else 1], (0, dy, 0))
+
+    stencil_load.wait()
     kc = (stencil[0, 0, 13] + stencil[1, 1, 13] + stencil[2, 2, 13]) / 3.0
     for c in range(3):
         rows = []
@@ -449,37 +508,49 @@
 
         lax.fori_loop(0, count // (16 * unroll), step, 0)
 
-    loads[5].wait()
+    windex_load.wait()
     for name in ("a", "b", "local"):
         build(windex, WIDE_SECTIONS[name], w, 2, None, 3)
-    for load in loads[6:]:
-        load.wait()
-
-    receive(ahead_first)
-    for n in range(3):
-        zmerged[n] = jnp.where((lane8 & 3) < 2, rz[1, n], rz[0, n])
-    on_first = send_on(zmerged, rf)
-
-    def along_z(own, passed, ox, oy):
-        return own[oy + 1] if ox == 0 else passed[0 if ox < 0 else 1, oy + 1]
+    for copy in rest:
+        copy.wait()
+    for name in ("coarse", "keep"):
+        build(cindex, COARSE_SECTIONS[name], w_coarse, 4, 144, 1)
+    for name in ("fine", "spread"):
+        build(findex, FINE_SECTIONS[name], w_fine, 2, 80, 3)
+
+    def along_z(slots, select, ox, oy):
+        return jnp.where(select, slots[1, ox + 1, oy + 1], slots[0, ox + 1, oy + 1])
+
+    from_high_1 = (lane8 & 3) < 2
+    from_high_2 = ((lane8 < 32) & ((lane8 & 1) == 0)) | ((lane8 >= 64) & (lane8 < 127))
 
     def wide_blocks(comp, tile):
         comps = 4
 
         def edge(ox, oy, k):
-            return roll(along_z(zmerged, rf, ox, oy), -4 * k)
+            return roll(along_z(rz, from_high_1, ox, oy), -4 * k)
 
         blocks = {}
         for p in range(4):
-            blocks[p] = edge(0, 0, p * comps + comp) if tile else main[p, comp]
+            own = main[p, comp] if comp < 3 else qmain[p]
+            blocks[p] = edge(0, 0, p * comps + comp) if tile else own
         for n in range(2):
-            blocks[n - 2] = edge(-1, 0, (n + 2) * comps + comp) if tile else rx[0, n, comp]
-            blocks[n + 4] = edge(1, 0, n * comps + comp) if tile else rx[1, n, comp]
+            for side, ox, first in ((0, -1, -2), (1, 1, 4)):
+                near = rx[side, n, comp] if comp < 3 else rqx[side, n]
+                plane = n if ox > 0 else n + 2
+                blocks[first + n] = edge(ox, 0, plane * comps + comp) if tile else near
         for s, oy in enumerate((-1, 1)):
             k = 4 * comps + (1 - s) * comps + comp
-            level, above, below = (edge(ox, oy, k) if tile else ry[s, ox + 1, comp] for ox in (0, 1, -1))
-            blocks["y", s] = level
-            blocks["c", s] = jnp.where(low_rows, above, below)
+            if tile:
+                blocks["y", s] = edge(0, oy, k)
+                blocks["c", s] = jnp.where(low_rows, edge(1, oy, k), edge(-1, oy, k))
+                continue
+            blocks["y", s] = ry[s, comp] if comp < 3 else rqy[s]
+            below, above = rc[0, s, comp // 2], rc[1, s, comp // 2]
+            if comp % 2 == 0:
+                blocks["c", s] = jnp.where(low_rows, above, below)
+            else:
+                blocks["c", s] = pltpu.roll(jnp.where(low_rows, below, above), 4, 0)
         return blocks
 
     def store_wide(target, comps, code_at, tile):
@@ -540,9 +611,9 @@
     def ring_inside():
         return inside(code256[ring_code : ring_code + 192, :])
 
-    receive(faces_first)
+    receive(1, plane_choices(2, 6, 3))
     store_wide(wide, (0, 1, 2), 0, 0)
-    receive(on_first)
+    receive(0, ahead_choices())
 
     store_wide(wide, (0, 1, 2), 0, 1)
     x2 = jnp.where(ring_inside(), gain_u * ring_of(wide, 3) + gain_s * operator_ring(), 0.0)
@@ -581,20 +652,36 @@
         last = (lane8 >= 32 + 4 * j) & (lane8 < 34 + 4 * j)
         total = jnp.where(first | last, roll(value, 98 + 4 * j), total)
         for p in range(4):
-            coarse[3 + j, 2 * p : 2 * p + 1, :] = before[p, j, 0:1, :]
-            coarse[3 + j, 2 * p + 1 : 2 * p + 2, :] = before[p, j, 7:8, :]
-    items = [before[p, j] for p in range(4) for j in range(3)] + [coarse[3 + j] for j in range(3)]
+            ysend[2 + j, 2 * p : 2 * p + 1, :] = before[p, j, 0:1, :]
+            ysend[2 + j, 2 * p + 1 : 2 * p + 2, :] = before[p, j, 7:8, :]
+            if p in (0, 3):
+                n = 0 if p == 0 else 1
+                xsend[n, 2 + j] = before[p, j]
+                csend[n, 2, 2 * j : 2 * j + 1, :] = before[p, j, 0:1, :]
+                csend[n, 2, 2 * j + 1 : 2 * j + 2, :] = before[p, j, 7:8, :]
+    items = [before[p, j] for p in range(4) for j in range(3)] + [ysend[2 + j] for j in range(3)]
     for k, value in enumerate(items):
         total = jnp.where(((lane8 + (129 - 2 * k)) & 127) < 2, roll(value, 2 * k), total)
     zpack2[...] = total
-    ahead_second = send_ahead(zpack2, rz2)
-    side = {offset: n for n, offset in enumerate(SIDES)}
-    sides_second = [
-        send(coarse, rs2.at[side[(-dx, -dy)]], (dx, dy, 0)) for dx, dy in SIDES
-    ]
+    for n, value in enumerate((jnp.where(lane8 < 64, coarse[0], roll(coarse[1], 64)), coarse[2])):
+        ysend[n] = value
+        for m in range(2):
+            xsend[m, n] = value
+            csend[m, n] = value
+    send_ahead(3, zpack2, rz2)
     for dx in (-1, 1):
-        sides_second.append(send(before.at[0 if dx < 0 else 3], rx2.at[0 if dx > 0 else 1], (dx, 0, 0)))
-
+        for dy in (-1, 1):
+            send(
+                4,
+                csend.at[0 if dx < 0 else 1],
+                rc2.at[0 if dx > 0 else 1, 0 if dy > 0 else 1],
+                (dx, dy, 0),
+            )
+        send(4, xsend.at[0 if dx < 0 else 1], rx2.at[0 if dx > 0 else 1], (dx, 0, 0))
+    for dy in (-1, 1):
+        send(4, ysend, ry2.at[0 if dy > 0 else 1], (0, dy, 0))
+
+    receive(2, plane_choices(0, 2, 1))
     store_wide(wide_p, (3,), wide_p_code, 0)
     store_wide(wide_p, (3,), wide_p_code, 1)
     q_ring = ring_of(wide_p, 1)
@@ -611,24 +698,21 @@
     p_out = (1.0 / 3.0) * p_in + (1.0 / 9.0) * q_in + (1.0 / 9.0) * near
     for p in range(4):
         pout_ref[p] = p_out[8 * p : 8 * p + 8, 0:128]
-    for name in ("coarse", "keep"):
-        build(cindex, COARSE_SECTIONS[name], w_coarse, 4, 144, 1)
-
-    receive(ahead_second)
-    from_high = ((lane8 < 32) & ((lane8 & 1) == 0)) | ((lane8 >= 64) & (lane8 < 127))
-    for n in range(3):
-        zmerged2[n] = jnp.where(from_high, rz2[1, n], rz2[0, n])
-    on_second = send_on(zmerged2, rf2)
-
-    for name in ("fine", "spread"):
-        build(findex, FINE_SECTIONS[name], w_fine, 2, 80, 3)
-
-    receive(sides_second)
-    receive(on_second)
+    receive(4, plane_choices(3, 5, 5))
+    receive(3, ahead_choices())
+
+    def from_side(ox, oy, n):
+        if ox and oy:
+            return rc2[0 if ox < 0 else 1, 0 if oy < 0 else 1, n]
+        return rx2[0 if ox < 0 else 1, n] if ox else ry2[0 if oy < 0 else 1, n]
 
     def coarse_block(ox, oy, j):
-        inner = coarse[j] if (ox, oy) == (0, 0) else rs2[side[(ox, oy)], j]
-        return jnp.where(lane8 < 64, inner, roll(along_z(zmerged2, rf2, ox, oy), -(34 + 4 * j)))
+        if (ox, oy) == (0, 0):
+            inner = coarse[j]
+        else:
+            inner = from_side(ox, oy, j // 2)
+            inner = roll(inner, 64) if j == 1 else inner
+        return jnp.where(lane8 < 64, inner, roll(along_z(rz2, from_high_2, ox, oy), -(34 + 4 * j)))
 
     blocks = []
     near_high = (row8 & 3) < 2
@@ -656,29 +740,33 @@
     product = jnp.dot(w_fine[...], right, preferred_element_type=F32)
 
     def ring_block(ox, oy, inner, k):
-        return jnp.concatenate([inner, roll(along_z(zmerged2, rf2, ox, oy), -2 * k)], axis=1)
-
-    def layer(ox, oy, j):
-        return ring_block(ox, oy, rs2[side[(ox, oy)], 3 + j], 12 + j)
+        return jnp.concatenate([inner, roll(along_z(rz2, from_high_2, ox, oy), -2 * k)], axis=1)
+
+    def layer(ox, j):
+        if ox == 0:
+            inner = jnp.where(odd_rows, from_side(0, -1, 2 + j), from_side(0, 1, 2 + j))
+        else:
+            inner = jnp.where(odd_rows, from_side(ox, -1, 2), from_side(ox, 1, 2))
+            shift = (-2 * j if ox > 0 else 6 - 2 * j) % 8
+            inner = pltpu.roll(inner, shift, 0) if shift else inner
+        outer = jnp.where(odd_rows, along_z(rz2, from_high_2, ox, -1), along_z(rz2, from_high_2, ox, 1))
+        return jnp.concatenate([inner, roll(outer, -2 * (12 + j))], axis=1)
 
     low_wide = lax.broadcasted_iota(jnp.int32, (8, 256), 0) < 4
-    odd_wide = (lax.broadcasted_iota(jnp.int32, (8, 256), 0) & 1) == 1
     halves = [[], []]
     for half in range(2):
         for x in ((-1, 0, 1), (2, 3, 4))[half]:
             for j in range(3):
                 if x == -1:
-                    halves[half].append(ring_block(-1, 0, rx2[0, j], 9 + j))
+                    halves[half].append(ring_block(-1, 0, rx2[0, 2 + j], 9 + j))
                 elif x == 4:
-                    halves[half].append(ring_block(1, 0, rx2[1, j], j))
+                    halves[half].append(ring_block(1, 0, rx2[1, 2 + j], j))
                 else:
                     halves[half].append(ring_block(0, 0, before[x, j], 3 * x + j))
     for j in range(3):
-        level = jnp.where(odd_wide, layer(0, -1, j), layer(0, 1, j))
-        low_x = jnp.where(odd_wide, layer(-1, -1, j), layer(-1, 1, j))
-        high_x = jnp.where(odd_wide, layer(1, -1, j), layer(1, 1, j))
-        halves[0].append(jnp.where(low_wide, level, low_x))
-        halves[1].append(jnp.where(low_wide, high_x, level))
+        level = layer(0, j)
+        halves[0].append(jnp.where(low_wide, level, layer(-1, j)))
+        halves[1].append(jnp.where(low_wide, layer(1, j), level))
     start = jnp.concatenate(halves[0] + halves[1], axis=0)
 
     down = ((1.0 / THETA) * ikc) * z_shift_sum(product, 192)
@@ -695,11 +783,11 @@
                 + (WEIGHT * ikc[:, 0:128]) * (main[p, j] - applied[n : n + 8, 0:128])
             )
 
-    for copy, there in sent:
-        pl.when(there)(copy.wait_send)
-
-
-COPIES = 6 + 8 + 2 + 6 + 10 + 2
+    for group, choices in groups:
+        wait_group(send_sem.at[group], choices)
+
+
+GROUPS = 5
 
 
 def scratch():
@@ -718,22 +806,28 @@
         vmem(FACE_1.shape, BF16),
         vmem(FACE_2.shape, BF16),
         vmem((4, 8, 128), F32),
-        vmem((4, 4, 8, 128), F32),
-        vmem((2, 4, 8, 128), F32),
+        vmem((4, 3, 8, 128), F32),
+        vmem((4, 8, 128), F32),
+        vmem((2, 3, 8, 128), F32),
+        vmem((2, 8, 128), F32),
+        vmem((2, 2, 2, 8, 128), F32),
         vmem((8, 128), F32),
+        vmem((2, 2, 3, 8, 128), F32),
+        vmem((2, 3, 8, 128), F32),
+        vmem((2, 2, 2, 8, 128), F32),
+        vmem((2, 2, 8, 128), F32),
+        vmem((2, 8, 128), F32),
+        vmem((2, 3, 3, 8, 128), F32),
+        vmem((4, 3, 8, 128), F32),
         vmem((3, 8, 128), F32),
-        vmem((2, 2, 4, 8, 128), F32),
-        vmem((2, 3, 4, 8, 128), F32),
+        vmem((8, 128), F32),
+        vmem((2, 5, 8, 128), F32),
+        vmem((5, 8, 128), F32),
         vmem((2, 3, 8, 128), F32),
-        vmem((2, 3, 8, 128), F32),
-        vmem((4, 3, 8, 128), F32),
-        vmem((6, 8, 128), F32),
-        vmem((8, 128), F32),
-        vmem((3, 8, 128), F32),
-        vmem((2, 3, 8, 128), F32),
-        vmem((8, 6, 8, 128), F32),
-        vmem((2, 3, 8, 128), F32),
-        vmem((2, 3, 8, 128), F32),
+        vmem((2, 5, 8, 128), F32),
+        vmem((2, 5, 8, 128), F32),
+        vmem((2, 2, 3, 8, 128), F32),
+        vmem((2, 3, 3, 8, 128), F32),
         vmem((9, 16, 128), F32),
         vmem((WIDE_ROWS, 768), BF16),
         vmem((COARSE_ROWS, 512), BF16),
@@ -742,9 +836,10 @@
         vmem((96, 256), F32),
         vmem((192, 256), F32),
         vmem((7, 32, 128), F32),
-        pltpu.SemaphoreType.DMA((12,)),
-        pltpu.SemaphoreType.DMA((COPIES,)),
-        pltpu.SemaphoreType.DMA((COPIES,)),
+        vmem((32, 8, 128), F32),
+        pltpu.SemaphoreType.DMA((10,)),
+        pltpu.SemaphoreType.DMA((GROUPS,)),
+        pltpu.SemaphoreType.DMA((GROUPS,)),
     ]
 
 

time: 32.2 us -> 28.7 us (0.89)
  Pallas kernels: 30.2 us -> 26.7 us
    pallas_call x1, Pallas kernels: 30.2 us -> 26.7 us  [on_device(): pl.pallas_call(body, name='stokes', out_shape=(pltpu.VMEM(rhs_velocity.sh...]
where the time goes in v2:
time: 28.7 us; the launch traced here: 28.6 us
  Pallas kernels  26.7 us (93%)
  local copies, waits for them, and re-layouts  1.23 us (4%)
  between operations  0.64 us (2%)
    pallas_call x1, Pallas kernels, on_device(): pl.pallas_call(body, name='stokes', out_shape=(pltpu.VMEM(rhs_velocity.sh...  26.7 us
    unnamed x2, local copies, waits for them, and re-layouts  1.23 us

profile of v2, /device:TPU:1, one launch (start us, length us, event | category | flops | bytes accessed | tf_op | source)
XLA Modules:
  0.0 28.6 jit_solution(6649858935787318252)
XLA Ops:
  0.6 26.7 %stokes.1 = (f32[3,4,8,128]{3,2,1,0:T(8,128)S(1)}, f32[4,8,128]{2,1,0:T(8,128)S(1)}) custom-call(f32[3,4,8,128]{3,2,1,0:T(8,128)} %rhs_hbm.1, f32[4,8,128]{2,1,0:T(8,128)} %press_hbm.1, s32[4,8,128]{2,1,0:T(8,128)} %ids_hbm.1, f32[8]{0:T(128)} %visc_hbm.1, f32[3,3,27]{2,1,0:T(4,128)} %bitcast.1, s32[288,256]{1,0:T(8,128)} %constant.14.clone.windex_hbm, ...), custom_call_target="tpu_custom_call" | custom-call | tf_op jit(solution)/shard_map/stokes/pallas_call | solution.py:849
  27.4 0.6 %copy.16 = f32[3,4,8,128]{3,2,1,0:T(8,128)} copy(f32[3,4,8,128]{3,2,1,0:T(8,128)S(1)} %get-tuple-element.2) | data formatting | bytes 98304
  28.0 0.6 %copy.17 = f32[4,8,128]{2,1,0:T(8,128)} copy(f32[4,8,128]{2,1,0:T(8,128)S(1)} %get-tuple-element.3) | data formatting | bytes 32768

commit v3 on v2

--- a/solution.py
+++ b/solution.py
@@ -843,10 +843,19 @@
     ]
 
 
+def store_results(velocity, pressure, velocity_out, pressure_out, sem):
+    one = pltpu.make_async_copy(velocity, velocity_out, sem.at[0])
+    two = pltpu.make_async_copy(pressure, pressure_out, sem.at[1])
+    one.start()
+    two.start()
+    one.wait()
+    two.wait()
+
+
 def on_device(rhs_velocity, rhs_pressure, layer_ids, visc_table, stencil):
     anywhere = pl.BlockSpec(memory_space=pltpu.HBM)
     inside = pl.BlockSpec(memory_space=pltpu.VMEM)
-    return pl.pallas_call(
+    results = pl.pallas_call(
         body,
         name="stokes",
         out_shape=(
@@ -878,6 +887,17 @@
             )
         )
     )
+    return pl.pallas_call(
+        store_results,
+        name="store",
+        out_shape=(
+            jax.ShapeDtypeStruct(rhs_velocity.shape, F32),
+            jax.ShapeDtypeStruct(rhs_pressure.shape, F32),
+        ),
+        in_specs=[inside] * 2,
+        out_specs=(anywhere,) * 2,
+        scratch_shapes=[pltpu.SemaphoreType.DMA((2,))],
+    )(*(pltpu.with_memory_space_constraint(value, pltpu.VMEM) for value in results))
 
 
 def solution(mesh):

time: 28.7 us -> 28.2 us (0.983)
  local copies, waits for them, and re-layouts: 1.23 us -> 0 us
  Pallas kernels: 26.7 us -> 27.4 us
    unnamed x2 -> x0, local copies, waits for them, and re-layouts: 1.23 us -> none
    pallas_call x0 -> x1, Pallas kernels: none -> 0.64 us  [on_device(): pl.pallas_call(store_results, name='store', out_shape=(jax.ShapeDtypeStru...]
where the time goes in v3:
time: 28.2 us; the launch traced here: 28 us
  Pallas kernels  27.4 us (97%)
  between operations  0.64 us (2%)
    pallas_call x1, Pallas kernels, on_device(): pl.pallas_call(body, name='stokes', out_shape=(pltpu.VMEM(rhs_velocity.sh...  26.7 us
    pallas_call x1, Pallas kernels, on_device(): pl.pallas_call(store_results, name='store', out_shape=(jax.ShapeDtypeStru...  0.64 us

profile of v3, /device:TPU:1, one launch (start us, length us, event | category | flops | bytes accessed | tf_op | source)
XLA Modules:
  0.0 28.0 jit_solution(1067908657002080667)
XLA Ops:
  0.6 26.7 %stokes.1 = (f32[3,4,8,128]{3,2,1,0:T(8,128)S(1)}, f32[4,8,128]{2,1,0:T(8,128)S(1)}) custom-call(f32[3,4,8,128]{3,2,1,0:T(8,128)} %rhs_hbm.1, f32[4,8,128]{2,1,0:T(8,128)} %press_hbm.1, s32[4,8,128]{2,1,0:T(8,128)} %ids_hbm.1, f32[8]{0:T(128)} %visc_hbm.1, f32[3,3,27]{2,1,0:T(4,128)} %bitcast.1, s32[288,256]{1,0:T(8,128)} %constant.14.clone.windex_hbm, ...), custom_call_target="tpu_custom_call" | custom-call | tf_op jit(solution)/shard_map/stokes/pallas_call | solution.py:858
  27.4 0.6 %store.1 = (f32[3,4,8,128]{3,2,1,0:T(8,128)}, f32[4,8,128]{2,1,0:T(8,128)}) custom-call(f32[3,4,8,128]{3,2,1,0:T(8,128)S(1)} %get-tuple-element.4.velocity, f32[4,8,128]{2,1,0:T(8,128)S(1)} %get-tuple-element.5.pressure), custom_call_target="tpu_custom_call" | custom-call | tf_op jit(solution)/shard_map/store/pallas_call | solution.py:890

commit v4 on v3

--- a/solution.py
+++ b/solution.py
@@ -289,17 +289,6 @@
     def device(dx, dy, dz):
         return (ix + dx, iy + dy, iz + dz)
 
-    partners = AHEAD + [(dx, dy, 0) for dx, dy in SIDES]
-    barrier = pltpu.get_barrier_semaphore()
-    expected = 0
-    for where in partners:
-        there = present(*where)
-        expected = expected + there.astype(jnp.int32)
-
-        @pl.when(there)
-        def _():
-            pl.semaphore_signal(barrier, inc=1, device_id=device(*where), device_id_type=MESH)
-
     def load(n, pairs):
         for source, target in pairs:
             pltpu.make_async_copy(source, target, in_sem.at[n]).start()
@@ -318,24 +307,27 @@
     windex_load = pltpu.make_async_copy(windex_hbm, windex, in_sem.at[3])
     windex_load.start()
     rest = [
-        pltpu.make_async_copy(source, target, in_sem.at[4 + n])
-        for n, (source, target) in enumerate(
-            [
-                (code256_hbm, code256), (code128_hbm, code128), (cindex_hbm, cindex), (findex_hbm, findex),
-                (face1_hbm, face1), (face2_hbm, face2),
-            ]
-        )
+        (code256_hbm, code256), (code128_hbm, code128), (cindex_hbm, cindex), (findex_hbm, findex),
+        (face1_hbm, face1), (face2_hbm, face2),
     ]
-    for copy in rest:
-        copy.start()
-
-    groups = []
+    load(4, rest)
+
+    partners = AHEAD + [(dx, dy, 0) for dx, dy in SIDES]
+    barrier = pltpu.get_barrier_semaphore()
+    expected = 0
+    for where in partners:
+        there = present(*where)
+        expected = expected + there.astype(jnp.int32)
+
+        @pl.when(there)
+        def _():
+            pl.semaphore_signal(barrier, inc=1, device_id=device(*where), device_id_type=MESH)
 
     def send(group, source, target, where):
         copy = pltpu.make_async_remote_copy(
             src_ref=source,
             dst_ref=target,
-            send_sem=send_sem.at[group],
+            send_sem=send_sem.at[0],
             recv_sem=recv_sem.at[group],
             device_id=device(*where),
             device_id_type=MESH,
@@ -376,7 +368,6 @@
 
     def receive(group, choices):
         wait_group(recv_sem.at[group], choices)
-        groups.append((group, choices))
 
     bad = NEVER
     for bit, end in (
@@ -511,8 +502,7 @@
     windex_load.wait()
     for name in ("a", "b", "local"):
         build(windex, WIDE_SECTIONS[name], w, 2, None, 3)
-    for copy in rest:
-        copy.wait()
+    loaded(4, REST_TILES)
     for name in ("coarse", "keep"):
         build(cindex, COARSE_SECTIONS[name], w_coarse, 4, 144, 1)
     for name in ("fine", "spread"):
@@ -567,7 +557,7 @@
         def block(n):
             return source[8 * comps * n : 8 * comps * (n + 1), :]
 
-        row = lax.broadcasted_iota(jnp.int32, (8 * comps, 256), 0)
+        row = lax.broadcasted_iota(jnp.int32, (8 * comps, source.shape[1]), 0)
         odd, low = (row & 1) == 1, (row & 7) < 4
         level = jnp.where(odd, block(5), block(6))
         corner = jnp.where(odd, block(7), block(8))
@@ -582,15 +572,17 @@
     def local_of(ring, comps):
         return jnp.concatenate([ring[8 * comps : 24 * comps], ring[32 * comps : 48 * comps]], axis=0)
 
-    def operator_ring():
+    def ring_products(tile):
+        lanes = slice(128 * tile, 128 * tile + 128)
         parts = []
         for name, start in (("a", 0), ("b", 32)):
-            high, low = split(wide[start : start + 256, :])
+            high, low = split(wide[start : start + 256, lanes])
             right = jnp.concatenate([high, high, low], axis=0)
             base = WIDE_SECTIONS[name][3]
-            product = jnp.dot(w[base : base + 288, :], right, preferred_element_type=F32)
-            parts.append(z_shift_sum(product, 96))
-        return jnp.concatenate(parts, axis=0)
+            parts.append(jnp.dot(w[base : base + 288, :], right, preferred_element_type=F32))
+        return tuple(
+            jnp.concatenate([part[96 * c : 96 * c + 96] for part in parts], axis=0) for c in range(3)
+        )
 
     def operator_local(value):
         high, low = split(value)
@@ -613,19 +605,36 @@
 
     receive(1, plane_choices(2, 6, 3))
     store_wide(wide, (0, 1, 2), 0, 0)
+
+    lane192 = lax.broadcasted_iota(jnp.int32, (192, 128), 1)
+    at_first, at_last = lane192 == 0, lane192 == 127
+    below, level, above = ring_products(0)
+    below, above = pltpu.roll(below, 1, 1), pltpu.roll(above, 127, 1)
+    gu, gs = gain_u[:, 0:128], gain_s[:, 0:128]
+    level = level + jnp.where(at_first, 0.0, below) + jnp.where(at_last, 0.0, above)
+    ring_x[:, 0:128] = gu * ring_of(wide[:, 0:128], 3) + gs * level
+    ring_x[:, 128:256] = gs * (jnp.where(at_first, below, 0.0) + jnp.where(at_last, above, 0.0))
+
     receive(0, ahead_choices())
-
     store_wide(wide, (0, 1, 2), 0, 1)
-    x2 = jnp.where(ring_inside(), gain_u * ring_of(wide, 3) + gain_s * operator_ring(), 0.0)
+    below, level, above = ring_products(1)
+    below, above = pltpu.roll(below, 1, 1), pltpu.roll(above, 127, 1)
+    one = ring_x[:, 0:128] + gs * jnp.where(at_first, below, jnp.where(at_last, above, 0.0))
+    two = level + jnp.where(at_last, below, jnp.where(at_first, above, 0.0))
+    two = ring_x[:, 128:256] + gu * ring_of(wide[:, 128:256], 3) + gs * two
+    x2 = jnp.where(ring_inside(), jnp.concatenate([one, two], axis=1), 0.0)
     ring_x[...] = x2
 
     applied = operator_local(x2)
     even = (lane8 * 2) & 127
 
-    def coarse_sum(source, n):
-        value = source[n, pl.ds(0, 8, 2), :] + source[n, pl.ds(1, 8, 2), :]
-        value = value + roll(value, -1)
-        return jnp.take_along_axis(value, even, axis=1, mode="promise_in_bounds")
+    def row_sum(source, n):
+        return source[n, pl.ds(0, 8, 2), :] + source[n, pl.ds(1, 8, 2), :]
+
+    def pair_sum(value, index):
+        one = jnp.take_along_axis(value, index, axis=1, mode="promise_in_bounds")
+        two = jnp.take_along_axis(value, index + 1, axis=1, mode="promise_in_bounds")
+        return one + two
 
     def local_row(p):
         return 8 * (3 + 3 * p if p < 2 else 6 + 3 * p)
@@ -643,14 +652,17 @@
                 before[p, j] = value
                 total = total + eta[p] * left
             resid[j, 8 * big : 8 * big + 8, :] = total
-    four_over = 4.0 / coarse_sum(resid, 3)
+    weights = row_sum(resid, 3)
+    four_over = 4.0 / pair_sum(weights, even)
     total = jnp.zeros((8, 128), F32)
     for j in range(3):
-        value = coarse_sum(resid, j) * four_over
-        coarse[j] = value
+        value = row_sum(resid, j)
+        coarse[j] = pair_sum(value, even) * four_over
         first = (lane8 >= 98 + 4 * j) & (lane8 < 100 + 4 * j)
         last = (lane8 >= 32 + 4 * j) & (lane8 < 34 + 4 * j)
-        total = jnp.where(first | last, roll(value, 98 + 4 * j), total)
+        here = jnp.where(first, 2 * (lane8 - (98 + 4 * j)), jnp.where(last, 2 * (lane8 + 30 - 4 * j), 0))
+        packed = pair_sum(value, here) * (4.0 / pair_sum(weights, here))
+        total = jnp.where(first | last, packed, total)
         for p in range(4):
             ysend[2 + j, 2 * p : 2 * p + 1, :] = before[p, j, 0:1, :]
             ysend[2 + j, 2 * p + 1 : 2 * p + 2, :] = before[p, j, 7:8, :]
@@ -783,11 +795,19 @@
                 + (WEIGHT * ikc[:, 0:128]) * (main[p, j] - applied[n : n + 8, 0:128])
             )
 
-    for group, choices in groups:
-        wait_group(send_sem.at[group], choices)
+    totals = [
+        (there, 2 * (nx + 1) * (ny + 1) * nz + 5 * nx * ny + 13 * nx + 9 * ny)
+        for (there, _), (nx, ny, nz) in zip(
+            ahead_choices(), [(nx, ny, nz) for nx in (1, 2) for ny in (1, 2) for nz in (1, 2)]
+        )
+    ]
+    wait_group(send_sem.at[0], totals)
 
 
 GROUPS = 5
+REST_TILES = (
+    CODE_256.size + CODE_128.size + COARSE_INDEX.size + FINE_INDEX.size + (FACE_1.size + FACE_2.size) // 2
+) // 1024
 
 
 def scratch():
@@ -836,9 +856,9 @@
         vmem((96, 256), F32),
         vmem((192, 256), F32),
         vmem((7, 32, 128), F32),
-        vmem((32, 8, 128), F32),
-        pltpu.SemaphoreType.DMA((10,)),
-        pltpu.SemaphoreType.DMA((GROUPS,)),
+        vmem((REST_TILES, 8, 128), F32),
+        pltpu.SemaphoreType.DMA((5,)),
+        pltpu.SemaphoreType.DMA((1,)),
         pltpu.SemaphoreType.DMA((GROUPS,)),
     ]
 

time: 28.2 us -> 28.4 us (level)
  no operation moved by 1% of the time
where the time goes in v4:
time: 28.4 us; the launch traced here: 28.3 us
  Pallas kernels  27.6 us (97%)
  between operations  0.64 us (2%)
    pallas_call x1, Pallas kernels, on_device(): pl.pallas_call(body, name='stokes', out_shape=(pltpu.VMEM(rhs_velocity.sh...  27 us
    pallas_call x1, Pallas kernels, on_device(): pl.pallas_call(store_results, name='store', out_shape=(jax.ShapeDtypeStru...  0.64 us

profile of v4, /device:TPU:1, one launch (start us, length us, event | category | flops | bytes accessed | tf_op | source)
XLA Modules:
  0.0 28.3 jit_solution(11538443803065654737)
XLA Ops:
  0.6 27.0 %stokes.1 = (f32[3,4,8,128]{3,2,1,0:T(8,128)S(1)}, f32[4,8,128]{2,1,0:T(8,128)S(1)}) custom-call(f32[3,4,8,128]{3,2,1,0:T(8,128)} %rhs_hbm.1, f32[4,8,128]{2,1,0:T(8,128)} %press_hbm.1, s32[4,8,128]{2,1,0:T(8,128)} %ids_hbm.1, f32[8]{0:T(128)} %visc_hbm.1, f32[3,3,27]{2,1,0:T(4,128)} %bitcast.1, s32[288,256]{1,0:T(8,128)} %constant.14.clone.windex_hbm, ...), custom_call_target="tpu_custom_call" | custom-call | tf_op jit(solution)/shard_map/stokes/pallas_call | solution.py:878
  27.6 0.6 %store.1 = (f32[3,4,8,128]{3,2,1,0:T(8,128)}, f32[4,8,128]{2,1,0:T(8,128)}) custom-call(f32[3,4,8,128]{3,2,1,0:T(8,128)S(1)} %get-tuple-element.4.velocity, f32[4,8,128]{2,1,0:T(8,128)S(1)} %get-tuple-element.5.pressure), custom_call_target="tpu_custom_call" | custom-call | tf_op jit(solution)/shard_map/store/pallas_call | solution.py:910

commit v5 on v4

--- a/solution.py
+++ b/solution.py
@@ -501,12 +501,8 @@
 
     windex_load.wait()
     for name in ("a", "b", "local"):
-        build(windex, WIDE_SECTIONS[name], w, 2, None, 3)
+        build(windex, WIDE_SECTIONS[name], w, 2, None, 6)
     loaded(4, REST_TILES)
-    for name in ("coarse", "keep"):
-        build(cindex, COARSE_SECTIONS[name], w_coarse, 4, 144, 1)
-    for name in ("fine", "spread"):
-        build(findex, FINE_SECTIONS[name], w_fine, 2, 80, 3)
 
     def along_z(slots, select, ox, oy):
         return jnp.where(select, slots[1, ox + 1, oy + 1], slots[0, ox + 1, oy + 1])
@@ -710,6 +706,10 @@
     p_out = (1.0 / 3.0) * p_in + (1.0 / 9.0) * q_in + (1.0 / 9.0) * near
     for p in range(4):
         pout_ref[p] = p_out[8 * p : 8 * p + 8, 0:128]
+    for name in ("coarse", "keep"):
+        build(cindex, COARSE_SECTIONS[name], w_coarse, 4, 144, 5)
+    for name in ("fine", "spread"):
+        build(findex, FINE_SECTIONS[name], w_fine, 2, 80, 6)
     receive(4, plane_choices(3, 5, 5))
     receive(3, ahead_choices())
 

time: 28.4 us -> 27.9 us (0.982)
  Pallas kernels: 27.6 us -> 27.1 us
    pallas_call x1, Pallas kernels: 27 us -> 26.4 us  [on_device(): pl.pallas_call(body, name='stokes', out_shape=(pltpu.VMEM(rhs_velocity.sh...]
where the time goes in v5:
time: 27.9 us; the launch traced here: 27.7 us
  Pallas kernels  27.1 us (97%)
  between operations  0.64 us (2%)
    pallas_call x1, Pallas kernels, on_device(): pl.pallas_call(body, name='stokes', out_shape=(pltpu.VMEM(rhs_velocity.sh...  26.4 us
    pallas_call x1, Pallas kernels, on_device(): pl.pallas_call(store_results, name='store', out_shape=(jax.ShapeDtypeStru...  0.64 us

profile of v5, /device:TPU:1, one launch (start us, length us, event | category | flops | bytes accessed | tf_op | source)
XLA Modules:
  0.0 27.7 jit_solution(12502491549620272565)
XLA Ops:
  0.6 26.4 %stokes.1 = (f32[3,4,8,128]{3,2,1,0:T(8,128)S(1)}, f32[4,8,128]{2,1,0:T(8,128)S(1)}) custom-call(f32[3,4,8,128]{3,2,1,0:T(8,128)} %rhs_hbm.1, f32[4,8,128]{2,1,0:T(8,128)} %press_hbm.1, s32[4,8,128]{2,1,0:T(8,128)} %ids_hbm.1, f32[8]{0:T(128)} %visc_hbm.1, f32[3,3,27]{2,1,0:T(4,128)} %bitcast.1, s32[288,256]{1,0:T(8,128)} %constant.14.clone.windex_hbm, ...), custom_call_target="tpu_custom_call" | custom-call | tf_op jit(solution)/shard_map/stokes/pallas_call | solution.py:878
  27.1 0.6 %store.1 = (f32[3,4,8,128]{3,2,1,0:T(8,128)}, f32[4,8,128]{2,1,0:T(8,128)}) custom-call(f32[3,4,8,128]{3,2,1,0:T(8,128)S(1)} %get-tuple-element.4.velocity, f32[4,8,128]{2,1,0:T(8,128)S(1)} %get-tuple-element.5.pressure), custom_call_target="tpu_custom_call" | custom-call | tf_op jit(solution)/shard_map/store/pallas_call | solution.py:910

commit v6 on v5

--- a/solution.py
+++ b/solution.py
@@ -568,17 +568,15 @@
     def local_of(ring, comps):
         return jnp.concatenate([ring[8 * comps : 24 * comps], ring[32 * comps : 48 * comps]], axis=0)
 
-    def ring_products(tile):
-        lanes = slice(128 * tile, 128 * tile + 128)
+    def operator_ring():
         parts = []
         for name, start in (("a", 0), ("b", 32)):
-            high, low = split(wide[start : start + 256, lanes])
+            high, low = split(wide[start : start + 256, :])
             right = jnp.concatenate([high, high, low], axis=0)
             base = WIDE_SECTIONS[name][3]
-            parts.append(jnp.dot(w[base : base + 288, :], right, preferred_element_type=F32))
-        return tuple(
-            jnp.concatenate([part[96 * c : 96 * c + 96] for part in parts], axis=0) for c in range(3)
-        )
+            product = jnp.dot(w[base : base + 288, :], right, preferred_element_type=F32)
+            parts.append(z_shift_sum(product, 96))
+        return jnp.concatenate(parts, axis=0)
 
     def operator_local(value):
         high, low = split(value)
@@ -602,23 +600,10 @@
     receive(1, plane_choices(2, 6, 3))
     store_wide(wide, (0, 1, 2), 0, 0)
 
-    lane192 = lax.broadcasted_iota(jnp.int32, (192, 128), 1)
-    at_first, at_last = lane192 == 0, lane192 == 127
-    below, level, above = ring_products(0)
-    below, above = pltpu.roll(below, 1, 1), pltpu.roll(above, 127, 1)
-    gu, gs = gain_u[:, 0:128], gain_s[:, 0:128]
-    level = level + jnp.where(at_first, 0.0, below) + jnp.where(at_last, 0.0, above)
-    ring_x[:, 0:128] = gu * ring_of(wide[:, 0:128], 3) + gs * level
-    ring_x[:, 128:256] = gs * (jnp.where(at_first, below, 0.0) + jnp.where(at_last, above, 0.0))
-
     receive(0, ahead_choices())
+
     store_wide(wide, (0, 1, 2), 0, 1)
-    below, level, above = ring_products(1)
-    below, above = pltpu.roll(below, 1, 1), pltpu.roll(above, 127, 1)
-    one = ring_x[:, 0:128] + gs * jnp.where(at_first, below, jnp.where(at_last, above, 0.0))
-    two = level + jnp.where(at_last, below, jnp.where(at_first, above, 0.0))
-    two = ring_x[:, 128:256] + gu * ring_of(wide[:, 128:256], 3) + gs * two
-    x2 = jnp.where(ring_inside(), jnp.concatenate([one, two], axis=1), 0.0)
+    x2 = jnp.where(ring_inside(), gain_u * ring_of(wide, 3) + gain_s * operator_ring(), 0.0)
     ring_x[...] = x2
 
     applied = operator_local(x2)

time: 27.9 us -> 27.4 us (0.982)
  Pallas kernels: 27.1 us -> 26.6 us
    pallas_call x1, Pallas kernels: 26.4 us -> 26 us  [on_device(): pl.pallas_call(body, name='stokes', out_shape=(pltpu.VMEM(rhs_velocity.sh...]
where the time goes in v6:
time: 27.4 us; the launch traced here: 27.3 us
  Pallas kernels  26.6 us (97%)
  between operations  0.64 us (2%)
    pallas_call x1, Pallas kernels, on_device(): pl.pallas_call(body, name='stokes', out_shape=(pltpu.VMEM(rhs_velocity.sh...  26 us
    pallas_call x1, Pallas kernels, on_device(): pl.pallas_call(store_results, name='store', out_shape=(jax.ShapeDtypeStru...  0.64 us

profile of v6, /device:TPU:1, one launch (start us, length us, event | category | flops | bytes accessed | tf_op | source)
XLA Modules:
  0.0 27.3 jit_solution(15985026707867826302)
XLA Ops:
  0.6 26.0 %stokes.1 = (f32[3,4,8,128]{3,2,1,0:T(8,128)S(1)}, f32[4,8,128]{2,1,0:T(8,128)S(1)}) custom-call(f32[3,4,8,128]{3,2,1,0:T(8,128)} %rhs_hbm.1, f32[4,8,128]{2,1,0:T(8,128)} %press_hbm.1, s32[4,8,128]{2,1,0:T(8,128)} %ids_hbm.1, f32[8]{0:T(128)} %visc_hbm.1, f32[3,3,27]{2,1,0:T(4,128)} %bitcast.1, s32[288,256]{1,0:T(8,128)} %constant.14.clone.windex_hbm, ...), custom_call_target="tpu_custom_call" | custom-call | tf_op jit(solution)/shard_map/stokes/pallas_call | solution.py:863
  26.6 0.6 %store.1 = (f32[3,4,8,128]{3,2,1,0:T(8,128)}, f32[4,8,128]{2,1,0:T(8,128)}) custom-call(f32[3,4,8,128]{3,2,1,0:T(8,128)S(1)} %get-tuple-element.4.velocity, f32[4,8,128]{2,1,0:T(8,128)S(1)} %get-tuple-element.5.pressure), custom_call_target="tpu_custom_call" | custom-call | tf_op jit(solution)/shard_map/store/pallas_call | solution.py:895

commit v7 on v6

--- a/solution.py
+++ b/solution.py
@@ -349,17 +349,17 @@
         return [
             (
                 jnp.logical_and(count_x == nx, count_y == ny),
-                corner * nx * ny + along_x * nx + along_y * ny,
+                2 * (corner * nx * ny + along_x * nx + along_y * ny),
             )
             for nx in (1, 2)
             for ny in (1, 2)
         ]
 
-    def ahead_choices():
+    def ahead_choices(corner):
         return [
             (
                 jnp.logical_and(jnp.logical_and(count_x == nx, count_y == ny), count_z == nz),
-                (nx + 1) * (ny + 1) * nz,
+                (2 + 2 * nx + 2 * ny + corner * nx * ny) * nz,
             )
             for nx in (1, 2)
             for ny in (1, 2)
@@ -387,7 +387,7 @@
         return pltpu.roll(value, shift % 128, 1) if shift % 128 else value
 
     visc_load.wait()
-    loaded(1, 20)
+    loaded(1, 40)
     for p in range(4):
         layer = ids[p]
         value = jnp.zeros((8, 128), F32)
@@ -423,7 +423,12 @@
 
     def send_ahead(group, source, slots):
         for dx, dy, dz in AHEAD:
-            send(group, source, slots.at[0 if dz > 0 else 1, 1 - dx, 1 - dy], (dx, dy, dz))
+            slot = slots.at[0 if dz > 0 else 1, 1 - dx, 1 - dy]
+            if group == 0 and dx and dy:
+                half = pl.ds(0 if dx < 0 else 4, 4)
+                send(group, source.at[half], slot.at[half], (dx, dy, dz))
+            else:
+                send(group, source, slot, (dx, dy, dz))
 
     send_ahead(0, zpack, rz)
     for dx in (-1, 1):
@@ -502,7 +507,7 @@
     windex_load.wait()
     for name in ("a", "b", "local"):
         build(windex, WIDE_SECTIONS[name], w, 2, None, 6)
-    loaded(4, REST_TILES)
+    loaded(4, 2 * REST_TILES)
 
     def along_z(slots, select, ox, oy):
         return jnp.where(select, slots[1, ox + 1, oy + 1], slots[0, ox + 1, oy + 1])
@@ -600,7 +605,7 @@
     receive(1, plane_choices(2, 6, 3))
     store_wide(wide, (0, 1, 2), 0, 0)
 
-    receive(0, ahead_choices())
+    receive(0, ahead_choices(1))
 
     store_wide(wide, (0, 1, 2), 0, 1)
     x2 = jnp.where(ring_inside(), gain_u * ring_of(wide, 3) + gain_s * operator_ring(), 0.0)
@@ -696,7 +701,7 @@
     for name in ("fine", "spread"):
         build(findex, FINE_SECTIONS[name], w_fine, 2, 80, 6)
     receive(4, plane_choices(3, 5, 5))
-    receive(3, ahead_choices())
+    receive(3, ahead_choices(2))
 
     def from_side(ox, oy, n):
         if ox and oy:
@@ -781,9 +786,9 @@
             )
 
     totals = [
-        (there, 2 * (nx + 1) * (ny + 1) * nz + 5 * nx * ny + 13 * nx + 9 * ny)
+        (there, (4 + 4 * nx + 4 * ny + 3 * nx * ny) * nz + 2 * (5 * nx * ny + 13 * nx + 9 * ny))
         for (there, _), (nx, ny, nz) in zip(
-            ahead_choices(), [(nx, ny, nz) for nx in (1, 2) for ny in (1, 2) for nz in (1, 2)]
+            ahead_choices(2), [(nx, ny, nz) for nx in (1, 2) for ny in (1, 2) for nz in (1, 2)]
         )
     ]
     wait_group(send_sem.at[0], totals)
@@ -841,7 +846,7 @@
         vmem((96, 256), F32),
         vmem((192, 256), F32),
         vmem((7, 32, 128), F32),
-        vmem((REST_TILES, 8, 128), F32),
+        vmem((2 * REST_TILES, 4, 128), F32),
         pltpu.SemaphoreType.DMA((5,)),
         pltpu.SemaphoreType.DMA((1,)),
         pltpu.SemaphoreType.DMA((GROUPS,)),

time: 27.4 us -> 27.4 us (level)
  no operation moved by 1% of the time
where the time goes in v7:
time: 27.4 us; the launch traced here: 27.2 us
  Pallas kernels  26.6 us (97%)
  between operations  0.64 us (2%)
    pallas_call x1, Pallas kernels, on_device(): pl.pallas_call(body, name='stokes', out_shape=(pltpu.VMEM(rhs_velocity.sh...  25.9 us
    pallas_call x1, Pallas kernels, on_device(): pl.pallas_call(store_results, name='store', out_shape=(jax.ShapeDtypeStru...  0.64 us

profile of v7, /device:TPU:1, one launch (start us, length us, event | category | flops | bytes accessed | tf_op | source)
XLA Modules:
  0.0 27.2 jit_solution(15583268353156715559)
XLA Ops:
  0.6 25.9 %stokes.1 = (f32[3,4,8,128]{3,2,1,0:T(8,128)S(1)}, f32[4,8,128]{2,1,0:T(8,128)S(1)}) custom-call(f32[3,4,8,128]{3,2,1,0:T(8,128)} %rhs_hbm.1, f32[4,8,128]{2,1,0:T(8,128)} %press_hbm.1, s32[4,8,128]{2,1,0:T(8,128)} %ids_hbm.1, f32[8]{0:T(128)} %visc_hbm.1, f32[3,3,27]{2,1,0:T(4,128)} %bitcast.1, s32[288,256]{1,0:T(8,128)} %constant.14.clone.windex_hbm, ...), custom_call_target="tpu_custom_call" | custom-call | tf_op jit(solution)/shard_map/stokes/pallas_call | solution.py:868
  26.6 0.6 %store.1 = (f32[3,4,8,128]{3,2,1,0:T(8,128)}, f32[4,8,128]{2,1,0:T(8,128)}) custom-call(f32[3,4,8,128]{3,2,1,0:T(8,128)S(1)} %get-tuple-element.4.velocity, f32[4,8,128]{2,1,0:T(8,128)S(1)} %get-tuple-element.5.pressure), custom_call_target="tpu_custom_call" | custom-call | tf_op jit(solution)/shard_map/store/pallas_call | solution.py:900
